TPU v7x, 32 devices: a whole 2x2x4 slice. The times are simulated.
32 devices in a mesh: dp: 8 (over z, x), tensor: 4 (over y, core).
Axes of the slice: x: 2, y: 2, z: 4, core: 2. Of those that a mesh axis runs over, the one named last changes fastest.
Arguments:
- tokens: bfloat16 [4096, 2560], P('dp'), may hold values from -6 to 6
- doc_start: int32 [4096], P('dp'), may hold values from 0 to 4095, as said below
- norm1_gain: float32 [2560], replicated, may hold values from 0.5 to 1.5
- proj_x: bfloat16 [2560, 2560], P(None, 'tensor'), may hold values from -0.125 to 0.125
- proj_y: bfloat16 [2560, 2560], P(None, 'tensor'), may hold values from -0.125 to 0.125
- conv_weight: float32 [4, 2560], P(None, 'tensor'), may hold values from -3 to 3
- conv_bias: float32 [2560], P('tensor'), may hold values from -2 to 2
- gate_x_weight: bfloat16 [256, 2560], P(None, 'tensor'), may hold values from -0.375 to 0.375
- gate_x_bias: float32 [2560], P('tensor'), may hold values from -4 to 4
- gate_a_weight: bfloat16 [256, 2560], P(None, 'tensor'), may hold values from -0.375 to 0.375
- gate_a_bias: float32 [2560], P('tensor'), may hold values from -4 to 4
- decay_param: float32 [2560], P('tensor'), as said below
- proj_out: bfloat16 [2560, 2560], P('tensor'), may hold values from -0.5 to 0.5
- norm2_gain: float32 [2560], replicated, may hold values from 0.5 to 1.5
- mlp_gate: bfloat16 [2560, 7680], P('dp', 'tensor'), may hold values from -0.125 to 0.125
- mlp_up: bfloat16 [2560, 7680], P('dp', 'tensor'), may hold values from -0.125 to 0.125
- mlp_down: bfloat16 [2560, 7680], P('dp', 'tensor'), may hold values from -0.125 to 0.125
- cotangent: bfloat16 [4096, 2560], P('dp'), may hold values from -6 to 6
Outputs:
- block_out: float32 [4096, 2560], P(('dp', 'tensor'))
- grad_tokens: float32 [4096, 2560], P(('dp', 'tensor'))
- grad_norm1_gain: float32 [2560], replicated
- grad_proj_x: float32 [2560, 2560], P('dp', 'tensor')
- grad_proj_y: float32 [2560, 2560], P('dp', 'tensor')
- grad_conv_weight: float32 [4, 2560], P(None, 'tensor')
- grad_conv_bias: float32 [2560], P('tensor')
- grad_gate_x_weight: float32 [256, 2560], P(None, 'tensor')
- grad_gate_x_bias: float32 [2560], P('tensor')
- grad_gate_a_weight: float32 [256, 2560], P(None, 'tensor')
- grad_gate_a_bias: float32 [2560], P('tensor')
- grad_decay_param: float32 [2560], P('tensor')
- grad_proj_out: float32 [2560, 2560], P('tensor', 'dp')
- grad_norm2_gain: float32 [2560], replicated
- grad_mlp_gate: float32 [2560, 7680], P('dp', 'tensor')
- grad_mlp_up: float32 [2560, 7680], P('dp', 'tensor')
- grad_mlp_down: float32 [2560, 7680], P('dp', 'tensor')
Inputs may be any that keep to these rules, and one draw needn't show every extreme that they name: `doc_start`: each token's entry is the stream position at which its document begins. Sequences of 2048 tokens begin at the positions 1792 + k * 2048, so the stream begins and ends with part of one; each begins a document. In each sequence the first document runs 3 * 512 to 2047 tokens and later ones 2048 // 10 to 2047 tokens, the last one cut at the sequence's end. `decay_param`: softplus of each entry lies between 0.02 / 2048 and 0.008.
All inputs are finite; a program needn't handle non-finite values.
Results may differ from a plain program's by a relative error of at most 0.025.
Values may be sent and summed in bfloat16 or wider, within the bound.
A program may use at most 448 MiB of HBM per device.

v0:
```python
import functools

import jax
import jax.numpy as jnp
from jax import lax
from jax.experimental import pallas as pl
from jax.experimental.pallas import tpu as pltpu
from jax.sharding import PartitionSpec as P


epsilon = 1e-06
MESH = pl.DeviceIdType.MESH
GROUP = 4
STRIP = 16
FIRST_BIT = 0
LINKS = (("dp", FIRST_BIT + 1), ("dp", FIRST_BIT), ("tensor", 1))
CORE = ("tensor", 0)
ORDERS = ((0, 1, 2), (0, 2, 1), (1, 2, 0), (2, 0, 1))
TILES = (8, 3, 5)
SUM_ORDERS = tuple(order[::-1] for order in ORDERS)
COLORS = range(len(ORDERS))


def gelu_tanh(values):
    return jax.nn.gelu(values, approximate=True)


def gated_product(gate_vals, up_vals):
    return gelu_tanh(gate_vals) * up_vals


def contract_last(left_rows, right_rows):
    return lax.dot_general(
        left_rows, right_rows, (((1,), (1,)), ((), ())), preferred_element_type=jnp.float32
    )


def contract_first(left_rows, right_rows):
    return lax.dot_general(
        left_rows, right_rows, (((0,), (0,)), ((), ())), preferred_element_type=jnp.float32
    )


def matmul(left_rows, right_rows):
    return jnp.dot(left_rows, right_rows, preferred_element_type=jnp.float32)


def shifted(block, axis, distance):
    devices = range(lax.axis_size(axis))
    route = [(i - distance, i) for i in devices if i - distance in devices]
    return lax.ppermute(block, axis, route)


def flipped(array, axis, mask):
    return lax.ppermute(array, axis, [(i, i ^ mask) for i in range(lax.axis_size(axis))])


def bit_of(axis, bit):
    return (lax.axis_index(axis) // (1 << bit)) % 2


def across(axis, bit):
    index = lax.axis_index(axis)
    return {axis: index + (1 - 2 * ((index // (1 << bit)) % 2)) * (1 << bit)}


def column_spans(width):
    tiles = width // 128
    counts = [tiles * part // 20 for part in TILES]
    spans, start = [], 0
    for count in (*counts, tiles - sum(counts)):
        spans.append((start * 128, count * 128))
        start += count
    return spans


def send(src, dst, send_sem, recv_sem, device):
    copy = pltpu.make_async_remote_copy(
        src_ref=src,
        dst_ref=dst,
        send_sem=send_sem,
        recv_sem=recv_sem,
        device_id=device,
        device_id_type=MESH,
    )
    copy.start()
    return copy


def greet(devices):
    barrier = pltpu.get_barrier_semaphore()
    for device in devices:
        pl.semaphore_signal(barrier, inc=1, device_id=device, device_id_type=MESH)
    pl.semaphore_wait(barrier, len(devices))


class Gather:
    def __init__(self, x_ref, out_ref, send_sem, recv_sem, core_send, core_recv, own_sem):
        self.sems = send_sem, recv_sem, core_send, core_recv
        self.out = out_ref
        self.me = [bit_of(*link) for link in LINKS]
        self.core = bit_of(*CORE)
        self.peers = [across(*link) for link in LINKS]
        self.core_peer = across(*CORE)
        self.spans = column_spans(x_ref.shape[1])
        me, place = self.me, out_ref.at[self.me[0], self.me[1], self.me[2], self.core]
        self.own = pltpu.make_async_copy(x_ref, place, own_sem)
        self.own.start()
        self.moving = [
            send(
                x_ref.at[:, pl.ds(*self.spans[k])],
                self.region(me, k),
                send_sem.at[k, 0],
                recv_sem.at[k, 0],
                self.peers[ORDERS[k][0]],
            )
            for k in COLORS
        ]
        self.to_core = [send(x_ref, place, core_send.at[3 * len(ORDERS)], core_recv.at[3 * len(ORDERS)], self.core_peer)]
        self.sent = []

    def region(self, idx, k):
        return self.out.at[idx[0], idx[1], idx[2], self.core, :, pl.ds(*self.spans[k])]

    def step(self, step):
        send_sem, recv_sem, core_send, core_recv = self.sems
        me = self.me
        if step == 0:
            self.own.wait()
        for k in COLORS:
            order = ORDERS[k]
            self.moving[k].wait_recv()
            self.sent.append(self.moving[k])
            if step < 2:
                held = [slice(None) if d in order[: step + 1] else me[d] for d in range(3)]
                self.moving[k] = send(
                    self.region(held, k),
                    self.region(held, k),
                    send_sem.at[k, step + 1],
                    recv_sem.at[k, step + 1],
                    self.peers[order[step + 1]],
                )
            fresh = [
                slice(None) if d in order[:step] else (1 - me[d] if d == order[step] else me[d])
                for d in range(3)
            ]
            self.to_core.append(
                send(
                    self.region(fresh, k),
                    self.region(fresh, k),
                    core_send.at[len(ORDERS) * step + k],
                    core_recv.at[len(ORDERS) * step + k],
                    self.core_peer,
                )
            )

    def finish(self):
        for copy in self.sent:
            copy.wait_send()
        for copy in self.to_core:
            copy.wait()


def spots_of_four():
    spot = lax.axis_index("dp") // (1 << FIRST_BIT) % GROUP
    return spot, spot + 1 - 2 * (spot % 2), spot + 2 - 4 * (spot // 2), GROUP - 1 - spot


def share_width(width):
    return -(-width // (128 * GROUP)) * 128


def overlap_of(width):
    return GROUP * share_width(width) - width


def cut_kernel(count, *refs):
    width = refs[0].shape[1]
    share, over = share_width(width), overlap_of(width)
    for spot, out in zip(spots_of_four(), refs[count:]):
        start = share * spot - over * (spot // (GROUP - 1))
        for i in range(count):
            out[i] = refs[i][:, pl.ds(pl.multiple_of(start, 128), share)]


def cut(*weights):
    rows, share = weights[0].shape[0], share_width(weights[0].shape[1])
    return pl.pallas_call(
        functools.partial(cut_kernel, len(weights)),
        name="cut",
        out_shape=[jax.ShapeDtypeStruct((len(weights), rows, share), jnp.bfloat16)] * GROUP,
        compiler_params=pltpu.CompilerParams(vmem_limit_bytes=24 * 2**20),
    )(*weights)


def place_kernel(count, *refs):
    for spot, piece in zip(spots_of_four(), refs[:GROUP]):
        for i in range(count):
            refs[GROUP + i][spot] = piece[i]


def placed(pieces):
    count, rows, share = pieces[0].shape
    return pl.pallas_call(
        functools.partial(place_kernel, count),
        name="place",
        out_shape=[jax.ShapeDtypeStruct((GROUP, rows, share), jnp.bfloat16)] * count,
        compiler_params=pltpu.CompilerParams(vmem_limit_bytes=24 * 2**20),
    )(*pieces)


class Collect:
    def __init__(self, part_ref, out_ref, slots, send_sem, recv_sem, own_sem):
        spot, *spots = spots_of_four()
        base = lax.axis_index("dp") - (spot << FIRST_BIT)
        self.out, self.slots = out_ref, slots
        self.copies = [
            send(
                part_ref.at[other],
                slots.at[spot],
                send_sem.at[m],
                recv_sem.at[m],
                {"dp": base + other * (1 << FIRST_BIT)},
            )
            for m, other in enumerate(spots)
        ]
        self.own = pltpu.make_async_copy(part_ref.at[spot], slots.at[spot], own_sem)
        self.own.start()

    def finish(self):
        self.own.wait()
        for copy in self.copies:
            copy.wait()
        rows, width = self.out.shape
        share, over = share_width(width), overlap_of(width)

        def strip(step, carry):
            at = pl.ds(pl.multiple_of(step * STRIP, STRIP), STRIP)
            for place in range(GROUP):
                skip = over * (place // (GROUP - 1))
                self.out[at, share * place : min(share * (place + 1), width)] = self.slots[
                    place, at, skip:share
                ].astype(jnp.float32)
            return carry

        lax.fori_loop(0, rows // STRIP, strip, 0)


def collect_scratch(rows, share):
    return [
        pltpu.VMEM((GROUP, rows, share), jnp.bfloat16),
        pltpu.SemaphoreType.DMA((GROUP - 1,)),
        pltpu.SemaphoreType.DMA((GROUP - 1,)),
        pltpu.SemaphoreType.DMA,
    ]


def exchanged(pieces):
    return [pieces[0]] + [flipped(pieces[m], "dp", m << FIRST_BIT) for m in range(1, GROUP)]


def final_kernel(
    n, bits, small_ref, gain1_ref, gain2_ref, all_ref, gains_ref, came, ssem, rsem, gs, gr
):
    place = lax.axis_index("dp")
    peers = [{"dp": (place + hop) % n} for hop in range(1, n)]
    greet(peers + [across("tensor", bit) for axis, bit in bits if axis == "tensor"])
    copies = [
        send(small_ref, all_ref.at[place], ssem.at[hop], rsem.at[hop], peers[hop])
        for hop in range(n - 1)
    ]
    all_ref[place] = small_ref[...]
    gains_ref[0:1] = gain1_ref[...]
    gains_ref[1:2] = gain2_ref[...]
    for step, (axis, bit) in enumerate(bits):
        copy = send(gains_ref, came.at[step], gs.at[step], gr.at[step], across(axis, bit))
        copy.wait()
        gains_ref[...] = gains_ref[...] + came[step]
    for copy in copies:
        copy.wait()


def final_pass(small, gain1, gain2):
    n = lax.axis_size("dp")
    bits = [
        (axis, bit)
        for axis in ("tensor", "dp")
        for bit in range(lax.axis_size(axis).bit_length() - 1)
    ]
    rows, width = small.shape
    vmem = pl.BlockSpec(memory_space=pltpu.VMEM)
    gains = (2, gain1.shape[1])
    return pl.pallas_call(
        functools.partial(final_kernel, n, bits),
        name="final",
        out_shape=(
            jax.ShapeDtypeStruct((n, rows, width), small.dtype),
            jax.ShapeDtypeStruct(gains, jnp.float32),
        ),
        in_specs=[vmem] * 3,
        out_specs=(vmem, vmem),
        scratch_shapes=[
            pltpu.VMEM((len(bits), *gains), jnp.float32),
            pltpu.SemaphoreType.DMA((n - 1,)),
            pltpu.SemaphoreType.DMA((n - 1,)),
            pltpu.SemaphoreType.DMA((len(bits),)),
            pltpu.SemaphoreType.DMA((len(bits),)),
        ],
        compiler_params=pltpu.CompilerParams(
            collective_id=8, has_side_effects=True, vmem_limit_bytes=24 * 2**20
        ),
    )(small, gain1, gain2)


GATHER_SEMS = [
    pltpu.SemaphoreType.DMA((len(ORDERS), 3)),
    pltpu.SemaphoreType.DMA((len(ORDERS), 3)),
    pltpu.SemaphoreType.DMA((3 * len(ORDERS) + 1,)),
    pltpu.SemaphoreType.DMA((3 * len(ORDERS) + 1,)),
    pltpu.SemaphoreType.DMA,
]


class SumTensor:
    def __init__(self, part_ref, q, core_buf, link_buf, sems_s, sems_r, own_sem):
        high, core = bit_of(*LINKS[2]), bit_of(*CORE)
        core_peer = across(*CORE)
        self.args = high, q, core_buf, link_buf, sems_s, sems_r
        self.own = pltpu.make_async_copy(part_ref.at[:, core], q, own_sem)
        self.own.start()
        self.copies = [
            send(
                part_ref.at[block, 1 - core],
                core_buf.at[block],
                sems_s.at[i],
                sems_r.at[i],
                core_peer,
            )
            for i, block in enumerate((1 - high, high))
        ]

    def pass_on(self):
        high, q, core_buf, link_buf, sems_s, sems_r = self.args
        self.own.wait()
        self.copies[0].wait_recv()
        q[1 - high] = q[1 - high] + core_buf[1 - high]
        self.copies.append(
            send(q.at[1 - high], link_buf, sems_s.at[2], sems_r.at[2], across(*LINKS[2]))
        )

    def arrive(self):
        self.copies[1].wait_recv()
        self.copies[2].wait_recv()

    def rows(self, rows):
        high, q, core_buf, link_buf, _, _ = self.args
        return (
            q[high, rows].astype(jnp.float32)
            + core_buf[high, rows].astype(jnp.float32)
            + link_buf[rows].astype(jnp.float32)
        )

    def finish(self):
        for copy in self.copies:
            copy.wait_send()


SUM_SEMS = [
    pltpu.SemaphoreType.DMA((3,)),
    pltpu.SemaphoreType.DMA((3,)),
    pltpu.SemaphoreType.DMA,
]


def middle_kernel(
    part_ref, tok_ref, cot_ref, gain_ref, resid_ref, all_ref, cot_all_ref,
    q, core_buf, link_buf, low, *sems
):
    greet([across(*link) for link in LINKS] + [across(*CORE)])
    total = SumTensor(part_ref, q, core_buf, link_buf, *sems[:3])
    total.pass_on()
    cots = Gather(cot_ref, cot_all_ref, *sems[8:])
    cots.step(0)
    total.arrive()

    def strip(i, carry):
        rows = pl.ds(pl.multiple_of(i * STRIP, STRIP), STRIP)
        resid = tok_ref[rows].astype(jnp.float32) + total.rows(rows)
        resid_ref[rows] = resid
        inv = lax.rsqrt(jnp.mean(resid * resid, axis=-1, keepdims=True) + epsilon)
        low[rows] = (resid * inv * gain_ref[...]).astype(low.dtype)
        return carry

    lax.fori_loop(0, tok_ref.shape[0] // STRIP, strip, 0)
    total.finish()
    blocks = Gather(low, all_ref, *sems[3:8])
    cots.step(1)
    blocks.step(0)
    blocks.step(1)
    cots.step(2)
    blocks.step(2)
    cots.finish()
    blocks.finish()


def middle(part, tok, cot, gain):
    rows, width = tok.shape
    vmem, anywhere = pl.BlockSpec(memory_space=pltpu.VMEM), pl.BlockSpec(memory_space=pl.ANY)
    return pl.pallas_call(
        middle_kernel,
        name="middle",
        out_shape=(
            jax.ShapeDtypeStruct((rows, width), jnp.float32),
            jax.ShapeDtypeStruct((2, 2, 2, 2, rows, width), jnp.bfloat16),
            jax.ShapeDtypeStruct((2, 2, 2, 2, rows, width), jnp.bfloat16),
        ),
        in_specs=[anywhere, vmem, vmem, vmem],
        out_specs=(vmem, anywhere, anywhere),
        scratch_shapes=[
            pltpu.VMEM((2, rows, width), jnp.bfloat16),
            pltpu.VMEM((2, rows, width), jnp.bfloat16),
            pltpu.VMEM((rows, width), jnp.bfloat16),
            pltpu.VMEM((rows, width), jnp.bfloat16),
            *SUM_SEMS,
            *GATHER_SEMS,
            *GATHER_SEMS,
        ],
        compiler_params=pltpu.CompilerParams(
            collective_id=1, has_side_effects=True, vmem_limit_bytes=32 * 2**20
        ),
    )(part.reshape(2, 2, rows, width), tok, cot, gain.reshape(1, width))


def norm_back(rows, back, base_ref, gain_ref, keep_ref, gain_acc):
    base = base_ref[rows].astype(jnp.float32)
    inv = lax.rsqrt(jnp.mean(base * base, axis=-1, keepdims=True) + epsilon)
    unit = base * inv
    scaled = gain_ref[...] * back
    grad = inv * (scaled - unit * jnp.mean(unit * scaled, axis=-1, keepdims=True))
    terms = back * unit
    gain_acc[...] += terms[:8] + terms[8:]
    return keep_ref[rows].astype(jnp.float32) + grad


def back_kernel(
    p_ref, resid_ref, cot_ref, gain_ref, grad_ref, all_ref, gain_out,
    q, cb, r0, r1, r2, low, gain_acc, ssem, rsem, fs, fr, own_sem, gs, gr, gather_own
):
    me = [bit_of(*link) for link in LINKS]
    core = bit_of(*CORE)
    peers = [across(*link) for link in LINKS]
    core_peer = across(*CORE)
    spans = column_spans(q.shape[-1])
    own = pltpu.make_async_copy(p_ref.at[:, :, :, core], q, own_sem)
    own.start()
    greet(peers + [core_peer])

    def half(k, near):
        first = SUM_ORDERS[k][0]
        return [(me[d] if near else 1 - me[d]) if d == first else slice(None) for d in range(3)]

    to_core = []
    for near in (False, True):
        for k in COLORS:
            i = half(k, near)
            to_core.append(
                send(
                    p_ref.at[i[0], i[1], i[2], 1 - core, :, pl.ds(*spans[k])],
                    cb.at[i[0], i[1], i[2], :, pl.ds(*spans[k])],
                    fs.at[len(to_core)],
                    fr.at[len(to_core)],
                    core_peer,
                )
            )
    own.wait()

    def add(i, k, other):
        s, n = spans[k]
        q[i[0], i[1], i[2], :, s : s + n] = q[i[0], i[1], i[2], :, s : s + n] + other

    moving, sent = [], []
    for near in (False, True):
        for k in COLORS:
            to_core[len(ORDERS) * near + k].wait_recv()
            i = half(k, near)
            s, n = spans[k]
            add(i, k, cb[i[0], i[1], i[2], :, s : s + n])
            if not near:
                moving.append(
                    send(
                        q.at[i[0], i[1], i[2], :, pl.ds(s, n)],
                        r0.at[:, :, :, pl.ds(s, n)],
                        ssem.at[k, 0],
                        rsem.at[k, 0],
                        peers[SUM_ORDERS[k][0]],
                    )
                )
    for step in (1, 2):
        for k in COLORS:
            s, n = spans[k]
            order = SUM_ORDERS[k]
            moving[k].wait_recv()
            sent.append(moving[k])
            kept = [me[d] if d in order[:step] else slice(None) for d in range(3)]
            add(kept, k, r0[:, :, :, s : s + n] if step == 1 else r1[:, :, s : s + n])
            away = [
                me[d] if d in order[:step] else (1 - me[d] if d == order[step] else slice(None))
                for d in range(3)
            ]
            moving[k] = send(
                q.at[away[0], away[1], away[2], :, pl.ds(s, n)],
                r1.at[:, :, pl.ds(s, n)] if step == 1 else r2.at[:, pl.ds(s, n)],
                ssem.at[k, step],
                rsem.at[k, step],
                peers[order[step]],
            )
    for k in COLORS:
        moving[k].wait_recv()
        sent.append(moving[k])
    gain_acc[...] = jnp.zeros_like(gain_acc)

    def strip(i, carry):
        rows = pl.ds(pl.multiple_of(i * STRIP, STRIP), STRIP)
        back = q[me[0], me[1], me[2], rows].astype(jnp.float32) + r2[rows].astype(jnp.float32)
        grad = norm_back(rows, back, resid_ref, gain_ref, cot_ref, gain_acc)
        grad_ref[rows] = grad
        low[rows] = grad.astype(low.dtype)
        return carry

    lax.fori_loop(0, low.shape[0] // STRIP, strip, 0)
    for copy in sent + to_core:
        copy.wait_send()
    gain_out[...] = jnp.sum(gain_acc[...], axis=0, keepdims=True)
    mine = all_ref.at[me[2], core]
    local = pltpu.make_async_copy(low, mine, gather_own)
    local.start()
    along = send(low, mine, gs.at[0], gr.at[0], peers[2])
    beside = send(low, mine, gs.at[1], gr.at[1], core_peer)
    along.wait_recv()
    theirs = all_ref.at[1 - me[2], core]
    onward = send(theirs, theirs, gs.at[2], gr.at[2], core_peer)
    local.wait()
    beside.wait()
    onward.wait()
    along.wait_send()


def back_pass(part, resid, cot, gain):
    rows, width = resid.shape
    wide = lambda *lead: pltpu.VMEM((*lead, rows, width), jnp.bfloat16)
    vmem = pl.BlockSpec(memory_space=pltpu.VMEM)
    return pl.pallas_call(
        back_kernel,
        name="back",
        out_shape=(
            jax.ShapeDtypeStruct((rows, width), jnp.float32),
            jax.ShapeDtypeStruct((2, 2, rows, width), jnp.bfloat16),
            jax.ShapeDtypeStruct((1, width), jnp.float32),
        ),
        in_specs=[pl.BlockSpec(memory_space=pl.ANY), vmem, vmem, vmem],
        out_specs=(vmem, pl.BlockSpec(memory_space=pl.ANY), vmem),
        scratch_shapes=[
            wide(2, 2, 2),
            wide(2, 2, 2),
            wide(2, 2),
            wide(2),
            wide(),
            wide(),
            pltpu.VMEM((8, width), jnp.float32),
            pltpu.SemaphoreType.DMA((len(ORDERS), 3)),
            pltpu.SemaphoreType.DMA((len(ORDERS), 3)),
            pltpu.SemaphoreType.DMA((2 * len(ORDERS),)),
            pltpu.SemaphoreType.DMA((2 * len(ORDERS),)),
            pltpu.SemaphoreType.DMA,
            pltpu.SemaphoreType.DMA((3,)),
            pltpu.SemaphoreType.DMA((3,)),
            pltpu.SemaphoreType.DMA,
        ],
        compiler_params=pltpu.CompilerParams(
            collective_id=2, has_side_effects=True, vmem_limit_bytes=40 * 2**20
        ),
    )(part.reshape(2, 2, 2, 2, rows, width), resid, cot, gain.reshape(1, width))


class Halve:
    def __init__(self, source, held, came, load_sem, send_sem, recv_sem, order, at_column=0):
        self.held, self.came, self.sems, self.order = held, came, (send_sem, recv_sem), order
        self.dims = sorted(order, reverse=True)
        self.sent, self.loads, at = [], [], 0
        lead = [slice(None) for _ in order]
        columns = pl.ds(at_column, held.shape[-1])
        for i, part in enumerate(source):
            rows = part.shape[-2]
            self.loads.append(
                pltpu.make_async_copy(
                    part.at[(*lead, slice(None), columns)],
                    held.at[(*lead, pl.ds(at, rows))],
                    load_sem.at[i],
                )
            )
            self.loads[-1].start()
            at += rows

    def index(self, done, away=None):
        picks = []
        for bit in self.dims:
            if bit in done:
                picks.append(bit_of("dp", bit))
            elif bit == away:
                picks.append(1 - bit_of("dp", bit))
            else:
                picks.append(slice(None))
        return tuple(picks)

    def start(self, step):
        if step == 0:
            for load in self.loads:
                load.wait()
        bit = self.order[step]
        self.moving = send(
            self.held.at[self.index(self.order[:step], bit)],
            self.came[step],
            self.sems[0].at[step],
            self.sems[1].at[step],
            across("dp", bit),
        )
        self.sent.append(self.moving)

    def land(self, step):
        self.moving.wait_recv()
        kept = self.index(self.order[: step + 1])
        self.held[kept] = self.held[kept] + self.came[step][...]
        if step + 1 < len(self.order):
            self.start(step + 1)

    def result(self):
        return self.held[self.index(self.order)]

    def finish(self):
        for copy in self.sent:
            copy.wait_send()


def halve_scratch(bits, rows, width):
    scratch = [pltpu.VMEM((*[2] * bits, rows, width), jnp.bfloat16)]
    for step in range(bits):
        scratch.append(pltpu.VMEM((*[2] * (bits - 1 - step), rows, width), jnp.bfloat16))
    return scratch + [
        pltpu.SemaphoreType.DMA((2,)),
        pltpu.SemaphoreType.DMA((bits,)),
        pltpu.SemaphoreType.DMA((bits,)),
    ]


def last_plan(bits, rows, few_rows, width):
    wide = width // 128 * 4 // 5 * 128
    swapped = [1, 0, *range(2, bits)]
    return [
        (list(range(bits)), 0, halve_scratch(bits, rows + few_rows, wide)),
        (swapped, wide, halve_scratch(bits, rows + few_rows, width - wide)),
        (list(range(1, bits)), 0, halve_scratch(bits - 1, rows, width)),
        ([0, *range(2, bits)], 0, halve_scratch(bits - 1, rows, width)),
    ]


def last_kernel(
    plan, part_ref, tok_ref, keep_ref, gain_ref, wide_ref, few_ref, y_ref, o_ref,
    row1_ref, row2_ref, row3_ref,
    grad_ref, gain_out, wide_out, few_out, y_out, o_out, row1_out, row2_out, row3_out,
    q, core_buf, link_buf, gain_acc, *refs
):
    sum_sems, refs = refs[:3], refs[3:]
    sources = ((wide_ref, few_ref), (wide_ref, few_ref), (y_ref,), (o_ref,))
    halvings = []
    for source, (order, column, scratch) in zip(sources, plan):
        mine, refs = refs[: len(scratch)], refs[len(scratch) :]
        came = mine[1 : 1 + len(order)]
        halvings.append(Halve(source, mine[0], came, *mine[1 + len(order) :], order, column))
    bits = len(plan[0][0])
    peers = [across("dp", bit) for bit in range(bits)]
    spot, *spots = spots_of_four()
    both = {"dp": lax.axis_index("dp") + (spots[2] - spot) * (1 << FIRST_BIT)}
    greet([across(*LINKS[2]), across(*CORE), both] + peers)
    total = SumTensor(part_ref, q, core_buf, link_buf, *sum_sems)
    for each in halvings:
        each.start(0)
    rows = zip((row1_ref, row2_ref, row3_ref), (row1_out, row2_out, row3_out))
    collects = [Collect(part, out, *refs[4 * i : 4 * i + 4]) for i, (part, out) in enumerate(rows)]
    total.pass_on()
    gain_acc[...] = jnp.zeros_like(gain_acc)

    def strip(i, carry):
        rows = pl.ds(pl.multiple_of(i * STRIP, STRIP), STRIP)
        back = total.rows(rows)
        grad_ref[rows] = norm_back(rows, back, tok_ref, gain_ref, keep_ref, gain_acc)
        return carry

    total.arrive()
    lax.fori_loop(0, tok_ref.shape[0] // STRIP, strip, 0)
    gain_out[...] = jnp.sum(gain_acc[...], axis=0, keepdims=True)
    for step in range(bits):
        for each in halvings:
            if step < len(each.order):
                each.land(step)
    rows = wide_out.shape[0]
    for each, (_, column, _) in zip(halvings[:2], plan):
        mine = each.result()
        columns = slice(column, column + mine.shape[1])
        wide_out[:, columns] = mine[:rows].astype(jnp.float32)
        few_out[:, columns] = mine[rows:]
    for each in collects:
        each.finish()
    y_out[...] = halvings[2].result().astype(jnp.float32)
    o_out[...] = halvings[3].result().astype(jnp.float32)
    for each in (*halvings, total):
        each.finish()


def last_pass(part, tok, keep, gain, wide, few, side_y, side_o, parts, hidden_width):
    rows, width = tok.shape
    vmem, anywhere = pl.BlockSpec(memory_space=pltpu.VMEM), pl.BlockSpec(memory_space=pl.ANY)
    bits = wide.shape[0].bit_length() - 1
    plan = last_plan(bits, wide.shape[1], few.shape[1], wide.shape[2])
    block = jax.ShapeDtypeStruct(wide.shape[1:], jnp.float32)
    leading = [2] * bits
    return pl.pallas_call(
        functools.partial(last_kernel, plan),
        name="last",
        out_shape=(
            jax.ShapeDtypeStruct((rows, width), jnp.float32),
            jax.ShapeDtypeStruct((1, width), jnp.float32),
            block,
            jax.ShapeDtypeStruct(few.shape[1:], jnp.bfloat16),
            block,
            block,
            *[jax.ShapeDtypeStruct((parts[0].shape[1], hidden_width), jnp.float32)] * 3,
        ),
        in_specs=[anywhere, vmem, vmem, vmem] + [anywhere] * 7,
        out_specs=(vmem,) * 9,
        scratch_shapes=[
            pltpu.VMEM((2, rows, width), jnp.bfloat16),
            pltpu.VMEM((2, rows, width), jnp.bfloat16),
            pltpu.VMEM((rows, width), jnp.bfloat16),
            pltpu.VMEM((8, width), jnp.float32),
            *SUM_SEMS,
            *[ref for _, _, scratch in plan for ref in scratch],
            *collect_scratch(*parts[0].shape[1:]) * 3,
        ],
        compiler_params=pltpu.CompilerParams(
            collective_id=3, has_side_effects=True, vmem_limit_bytes=48 * 2**20
        ),
    )(
        part.reshape(2, 2, rows, width),
        tok,
        keep,
        gain.reshape(1, width),
        wide.reshape(*leading, *wide.shape[1:]),
        few.reshape(*leading, *few.shape[1:]),
        side_y,
        side_o,
        *parts,
    )


def scan_kernel(n, reverse, *refs):
    a_ref, b_ref, out_ref, edge_ref, fa, fb, mine, others, ssem, rsem = refs
    place = lax.axis_index("dp")
    sign = -1 if reverse else 1
    barrier = pltpu.get_barrier_semaphore()
    peers = [{"dp": (place + sign * hop + n) % n} for hop in range(1, n)]
    for peer in peers:
        pl.semaphore_signal(barrier, inc=1, device_id=peer, device_id_type=MESH)
    rows, width = a_ref.shape
    length = rows // 8
    lanes = range(width // 128)
    for k in lanes:
        fa[k * rows : (k + 1) * rows] = a_ref[:, k * 128 : (k + 1) * 128]
        fb[k * rows : (k + 1) * rows] = b_ref[:, k * 128 : (k + 1) * 128]

    def at(k, r):
        return pl.ds(k * rows + (length - 1 - r if reverse else r), 8, stride=length)

    def local(r, carry):
        result = []
        for k in lanes:
            prod, state = carry[k]
            decay = fa[at(k, r), :]
            term = fb[at(k, r), :]
            if reverse:
                fa[at(k, r), :] = prod
                total = term + state
                fb[at(k, r), :] = total
                result.append((prod * decay, decay * total))
            else:
                prod = prod * decay
                state = decay * state + term
                fa[at(k, r), :] = prod
                fb[at(k, r), :] = state
                result.append((prod, state))
        return result

    start = [(jnp.ones((8, 128), jnp.float32), jnp.zeros((8, 128), jnp.float32)) for k in lanes]
    ends = lax.fori_loop(0, length, local, start, unroll=2)
    prod = jnp.concatenate([end[0] for end in ends], axis=1)
    state = jnp.concatenate([end[1] for end in ends], axis=1)
    order = range(7, -1, -1) if reverse else range(8)
    run_a, run_b = jnp.ones((1, width), jnp.float32), jnp.zeros((1, width), jnp.float32)
    before = [None] * 8
    for s in order:
        before[s] = (run_a, run_b)
        pa, pb = prod[s : s + 1], state[s : s + 1]
        run_a, run_b = pa * run_a, pa * run_b + pb
    mine[0:1] = run_a
    mine[1:2] = run_b
    pl.semaphore_wait(barrier, n - 1)
    copies = [
        send(mine, others.at[hop - 1], ssem.at[hop - 1], rsem.at[hop - 1], peers[hop - 1])
        for hop in range(1, n)
    ]
    carry = jnp.zeros((1, width), jnp.float32)
    ahead = n - 1 - place if reverse else place
    for copy in copies:
        copy.wait_recv()
    for hop in range(n - 1, 0, -1):
        step = others[hop - 1, 0:1] * carry + others[hop - 1, 1:2]
        carry = jnp.where(hop <= ahead, step, carry)
    edge_ref[...] = carry
    entering = jnp.concatenate([pa * carry + pb for pa, pb in before], axis=0)

    def fix(r, c):
        for k in lanes:
            fb[at(k, r), :] = fb[at(k, r), :] + fa[at(k, r), :] * entering[:, k * 128 : (k + 1) * 128]
        return c

    lax.fori_loop(0, length, fix, 0, unroll=2)
    for k in lanes:
        out_ref[:, k * 128 : (k + 1) * 128] = fb[k * rows : (k + 1) * rows]
    for copy in copies:
        copy.wait_send()


def scan_stream(decay, term, reverse):
    n = lax.axis_size("dp")
    rows, width = decay.shape
    vmem = pl.BlockSpec(memory_space=pltpu.VMEM)
    return pl.pallas_call(
        functools.partial(scan_kernel, n, reverse),
        name="scan_back" if reverse else "scan",
        out_shape=(
            jax.ShapeDtypeStruct((rows, width), jnp.float32),
            jax.ShapeDtypeStruct((1, width), jnp.float32),
        ),
        in_specs=[vmem, vmem],
        out_specs=(vmem, vmem),
        scratch_shapes=[
            pltpu.VMEM((rows * width // 128, 128), jnp.float32),
            pltpu.VMEM((rows * width // 128, 128), jnp.float32),
            pltpu.VMEM((2, width), jnp.float32),
            pltpu.VMEM((n - 1, 2, width), jnp.float32),
            pltpu.SemaphoreType.DMA((n - 1,)),
            pltpu.SemaphoreType.DMA((n - 1,)),
        ],
        compiler_params=pltpu.CompilerParams(
            collective_id=5 if reverse else 4, has_side_effects=True, vmem_limit_bytes=32 * 2**20
        ),
    )(decay, term)


def in_order(bit, mine, theirs, axis=0):
    return jnp.where(
        bit == 0, jnp.concatenate([mine, theirs], axis), jnp.concatenate([theirs, mine], axis)
    )


def parted(held, dims, bit):
    mine = (lax.axis_index("dp") >> bit) % 2
    axis = dims.index(bit)
    return (
        lax.dynamic_index_in_dim(held, mine, axis, False),
        lax.dynamic_index_in_dim(held, 1 - mine, axis, False),
    )


def added(keep, came):
    return (keep.astype(jnp.float32) + came.astype(jnp.float32)).astype(jnp.bfloat16)


def inner(
    tokens,
    doc_start,
    norm1_gain,
    proj_x,
    proj_y,
    conv_weight,
    conv_bias,
    gate_x_weight,
    gate_x_bias,
    gate_a_weight,
    gate_a_bias,
    decay_param,
    proj_out,
    norm2_gain,
    mlp_gate,
    mlp_up,
    mlp_down,
    cotangent,
):
    tok_rows = tokens.shape[0]
    chan_width = proj_x.shape[1]
    block_width = gate_x_weight.shape[0]
    half_width = block_width // 2
    tap_count = conv_weight.shape[0]
    parity = lax.axis_index("tensor") % 2
    full_start = parity * half_width
    shared_start = (1 - parity) * 2 * block_width
    tensor_size = lax.axis_size("tensor")
    share_rows = tok_rows // tensor_size
    own_start = lax.axis_index("tensor") * share_rows
    positions = lax.axis_index("dp") * tok_rows + lax.iota(jnp.int32, tok_rows)
    starting = (doc_start == positions)[:, None]
    dp_size = lax.axis_size("dp")
    low_size = 1 << FIRST_BIT
    high_size = dp_size // (GROUP * low_size)

    def dp_index(high, four, low):
        return (high * GROUP + four) * low_size + low

    highs, fours, lows = range(high_size), range(GROUP), range(low_size)
    groups = [
        [dp_index(h, i, l) * tensor_size + t for i in fours for t in range(tensor_size)]
        for h in highs
        for l in lows
    ]
    low_groups = [[dp_index(h, i, l) for l in lows] for h in highs for i in fours]
    high_groups = [[dp_index(h, i, l) for h in highs] for i in fours for l in lows]
    everyone = ("dp", "tensor")

    spot = lax.axis_index("dp") // low_size % GROUP
    hidden_width = mlp_gate.shape[1]
    share = share_width(hidden_width)

    def all_rows(part):
        rows = part.shape[1]
        if low_size > 1:
            part = lax.all_gather(
                part[:, None], "dp", axis=1, axis_index_groups=low_groups, tiled=True
            )
        if high_size > 1:
            part = lax.all_gather(part, "dp", axis=0, axis_index_groups=high_groups, tiled=True)
        return part.reshape(dp_size * rows, share)

    def own_rows(grad):
        rows = grad.shape[0] // dp_size
        grad = grad.astype(jnp.bfloat16).reshape(high_size * GROUP, low_size, rows, share)
        if high_size > 1:
            grad = lax.psum_scatter(
                grad, "dp", axis_index_groups=high_groups, scatter_dimension=0, tiled=True
            )
        if low_size > 1:
            grad = lax.psum_scatter(
                grad, "dp", axis_index_groups=low_groups, scatter_dimension=1, tiled=True
            )
        return grad.reshape(GROUP, rows, share)

    cot_own = lax.dynamic_slice_in_dim(cotangent, own_start, share_rows, 0)
    gate_pieces = exchanged(cut(mlp_gate))
    pieces = exchanged(cut(mlp_up, mlp_down))
    tok_own = lax.dynamic_slice_in_dim(tokens, own_start, share_rows, 0)

    def normalize(values):
        values = values.astype(jnp.float32)
        inv_rms = lax.rsqrt(jnp.mean(values * values, axis=-1, keepdims=True) + epsilon)
        return (values * inv_rms * norm1_gain).astype(jnp.bfloat16)

    halo = 16
    normed_low = normalize(tokens)
    normed_low, *gate_pieces = lax.optimization_barrier((normed_low, *gate_pieces))
    gate_cols = all_rows(*placed(gate_pieces))
    normed_prev = normalize(shifted(tokens[tok_rows - halo :], "dp", 1))
    branch_y = matmul(normed_low, proj_y)
    branch_x = matmul(normed_low, proj_x).astype(jnp.bfloat16)
    prev_x = matmul(normed_prev, proj_x).astype(jnp.bfloat16)
    extended = jnp.concatenate([prev_x[halo - tap_count + 1 :], branch_x], axis=0).astype(
        jnp.float32
    )

    def conv_apply(ext_rows, weight, bias_vec):
        conv_out = bias_vec + weight[0] * ext_rows[tap_count - 1 :]
        for offset in range(1, tap_count):
            inside = (positions - offset >= doc_start).astype(jnp.float32)[:, None]
            lagged = ext_rows[tap_count - 1 - offset : tap_count - 1 - offset + tok_rows]
            conv_out = conv_out + weight[offset] * lagged * inside
        return conv_out

    conv_out, conv_pull = jax.vjp(conv_apply, extended, conv_weight, conv_bias)
    mixed_low = conv_out.astype(jnp.bfloat16)
    own_half = lax.dynamic_slice_in_dim(mixed_low, shared_start, half_width, 1)
    other_half = flipped(own_half, "tensor", 1)
    shared_in = in_order(parity, own_half, other_half, 1)
    full_in = lax.dynamic_slice_in_dim(mixed_low, full_start, 2 * block_width, 1).reshape(
        tok_rows, 2, block_width
    )

    def place(full_part, shared_part):
        return in_order(parity, full_part, shared_part, 1)

    def full_weight(weight):
        return lax.dynamic_slice_in_dim(weight, full_start, 2 * block_width, 1).reshape(
            block_width, 2, block_width
        )

    def shared_weight(weight):
        return lax.dynamic_slice_in_dim(weight, shared_start, half_width, 1)

    def gate_pre(weight, bias_vec):
        full_out = jnp.einsum(
            "nhi,ihj->nhj", full_in, full_weight(weight), preferred_element_type=jnp.float32
        ).reshape(tok_rows, 2 * block_width)
        shared_out = matmul(shared_in, shared_weight(weight))
        return place(full_out, shared_out) + bias_vec

    def recurrence_in(conv_vals, pre_input, pre_recur, param_vec):
        log_decay = -8.0 * jax.nn.sigmoid(pre_recur) * jax.nn.softplus(param_vec)
        decay = jnp.where(starting, 0.0, jnp.exp(log_decay))
        multiplier = jnp.where(starting, 1.0, jnp.sqrt(-jnp.expm1(2.0 * log_decay)))
        return (decay, multiplier * jax.nn.sigmoid(pre_input) * conv_vals)

    pre_input = gate_pre(gate_x_weight, gate_x_bias)
    pre_recur = gate_pre(gate_a_weight, gate_a_bias)
    (decay, drive), recur_pull = jax.vjp(
        recurrence_in, mixed_low.astype(jnp.float32), pre_input, pre_recur, decay_param
    )
    decay, drive, *pieces = lax.optimization_barrier((decay, drive, *pieces))
    up_cols, down_cols = (all_rows(part) for part in placed(pieces))
    states, entering = scan_stream(decay, drive, False)
    previous = jnp.concatenate([entering, states[:-1]], axis=0)
    gelu_y, gelu_pull = jax.vjp(gelu_tanh, branch_y)
    product_low = (states * gelu_y).astype(jnp.bfloat16)
    lru_part = matmul(product_low, proj_out).astype(jnp.bfloat16)
    resid, normed2_all, cot_all = middle(lru_part, tok_own, cot_own, norm2_gain)
    cot_all = cot_all.reshape(GROUP * tok_rows, -1)
    normed2_all = normed2_all.reshape(GROUP * tok_rows, -1)
    counted = lax.iota(jnp.int32, share) >= overlap_of(hidden_width) * (spot // (GROUP - 1))

    def once(values):
        return jnp.where(counted, values, 0.0).astype(jnp.bfloat16)

    gate_act = matmul(normed2_all, gate_cols)
    up_act = matmul(normed2_all, up_cols)
    hidden, act_pull = jax.vjp(gated_product, gate_act, up_act)
    hidden_low = once(hidden)
    grad_hidden = matmul(cot_all, down_cols)
    grad_gate, grad_up = act_pull(grad_hidden)
    grad_gate_low = once(grad_gate)
    grad_up_low = once(grad_up)

    out_part = contract_last(hidden_low, down_cols).astype(jnp.bfloat16)
    out_part, hidden_low, grad_gate_low, grad_up_low = lax.optimization_barrier(
        (out_part, hidden_low, grad_gate_low, grad_up_low)
    )
    back_part = (
        contract_last(grad_gate_low, gate_cols) + contract_last(grad_up_low, up_cols)
    ).astype(jnp.bfloat16)
    down_grad = contract_first(cot_all, hidden_low).astype(jnp.bfloat16)
    back_part, down_grad = lax.optimization_barrier((back_part, down_grad))
    down_rows = own_rows(down_grad)
    grad_resid, grad_lru_low, grad_gain2 = back_pass(back_part, resid, cot_own, norm2_gain)
    grad_lru_low = grad_lru_low.reshape(tok_rows, -1)
    gate_rows = own_rows(contract_first(normed2_all, grad_gate_low))
    up_rows = own_rows(contract_first(normed2_all, grad_up_low))
    block_out = resid + lax.psum_scatter(
        out_part,
        everyone,
        axis_index_groups=groups,
        scatter_dimension=0,
        tiled=True,
    ).astype(jnp.float32)

    grad_product = contract_last(grad_lru_low, proj_out)
    grad_states = grad_product * gelu_y
    grad_y_low = gelu_pull(grad_product * states)[0].astype(jnp.bfloat16)
    total_grad, _ = scan_stream(decay, grad_states, True)
    total_grad, late_y, late_lru = lax.optimization_barrier(
        (total_grad, grad_y_low, grad_lru_low)
    )

    def token_sum(left_rows, right_rows):
        return contract_first(left_rows, right_rows).astype(jnp.bfloat16)

    def per_device(rows):
        return rows.reshape(dp_size, rows.shape[0] // dp_size, rows.shape[1])

    dims = list(range(dp_size.bit_length() - 1))[::-1]

    def by_bits(grad):
        return grad.reshape(*[2] * len(dims), grad.shape[0] // dp_size, grad.shape[1])

    keep_y, away_y = parted(by_bits(token_sum(normed_low, late_y)), dims, 0)
    keep_o, away_o = parted(by_bits(token_sum(late_lru, product_low)), dims, 1)
    total_grad, away_y, away_o = lax.optimization_barrier((total_grad, away_y, away_o))
    came_y, came_o = flipped(away_y, "dp", 1), flipped(away_o, "dp", 2)
    back_y = contract_last(late_y, proj_y)
    conv_direct, grad_pre_input, grad_pre_recur, grad_param = recur_pull(
        (total_grad * previous, total_grad)
    )

    def gate_back(weight, grad_pre):
        grad_pre_low = grad_pre.astype(jnp.bfloat16)
        grad_full = lax.dynamic_slice_in_dim(grad_pre_low, full_start, 2 * block_width, 1).reshape(
            tok_rows, 2, block_width
        )
        grad_share = lax.dynamic_slice_in_dim(grad_pre_low, shared_start, half_width, 1)
        into_full = jnp.einsum(
            "nhj,ihj->nhi", grad_full, full_weight(weight), preferred_element_type=jnp.float32
        ).reshape(tok_rows, 2 * block_width)
        into_share = contract_last(grad_share, shared_weight(weight))
        weight_full = jnp.einsum(
            "nhi,nhj->ihj", full_in, grad_full, preferred_element_type=jnp.float32
        ).reshape(block_width, 2 * block_width)
        weight_share = contract_first(shared_in, grad_share)
        return (into_full, into_share, place(weight_full, weight_share))

    input_full, input_share, grad_gx_weight = gate_back(gate_x_weight, grad_pre_input)
    recur_full, recur_share, grad_ga_weight = gate_back(gate_a_weight, grad_pre_recur)
    full_sum = input_full + recur_full
    share_sum = input_share + recur_share
    own_grad = jnp.where(parity == 0, share_sum[:, :half_width], share_sum[:, half_width:])
    other_grad = jnp.where(parity == 0, share_sum[:, half_width:], share_sum[:, :half_width])
    returned = flipped(other_grad.astype(jnp.bfloat16), "tensor", 1).astype(other_grad.dtype)
    grad_conv = conv_direct + place(full_sum, own_grad + returned)
    grad_extended, grad_conv_weight, grad_conv_bias = conv_pull(grad_conv)
    rim_rows, came_y, came_o = lax.optimization_barrier(
        (grad_extended[: tap_count - 1], came_y, came_o)
    )
    side_y, side_o = added(keep_y, came_y), added(keep_o, came_o)
    rim_grad = shifted(rim_rows, "dp", -1)
    grad_branch_x = grad_extended[tap_count - 1 :] + jnp.concatenate(
        [jnp.zeros((tok_rows - tap_count + 1, chan_width), jnp.float32), rim_grad], axis=0
    )
    grad_x_low = grad_branch_x.astype(jnp.bfloat16)
    wide = jnp.concatenate([grad_gx_weight, grad_ga_weight], axis=0)
    sums = jnp.concatenate(
        [
            grad_conv_weight,
            grad_conv_bias[None],
            jnp.sum(grad_pre_input, axis=0)[None],
            jnp.sum(grad_pre_recur, axis=0)[None],
            grad_param[None],
        ],
        axis=0,
    )
    spare = dp_size * 16 - sums.shape[0]
    sums = jnp.concatenate([sums, jnp.zeros((spare, chan_width), jnp.float32)], axis=0)
    few = jnp.concatenate(
        [per_device(wide.astype(jnp.bfloat16)), per_device(sums.astype(jnp.bfloat16))], axis=1
    )
    grad_tokens, grad_gain1, grad_proj_x, reduced, grad_proj_y, grad_out, *grad_rows = last_pass(
        (contract_last(grad_x_low, proj_x) + back_y).astype(jnp.bfloat16),
        tok_own,
        grad_resid,
        norm1_gain,
        per_device(token_sum(normed_low, grad_x_low)),
        few,
        side_y,
        side_o,
        (down_rows, gate_rows, up_rows),
        hidden_width,
    )
    grad_mlp_down, grad_mlp_gate, grad_mlp_up = grad_rows
    grad_proj_out = grad_out.T
    shared, gains = final_pass(reduced, grad_gain1, grad_gain2)
    wide_rows = 2 * block_width // dp_size
    wide = shared[:, :wide_rows].reshape(2 * block_width, chan_width).astype(jnp.float32)
    small = shared[:, wide_rows:].reshape(dp_size * 16, chan_width).astype(jnp.float32)
    return (
        block_out,
        grad_tokens,
        gains[0],
        grad_proj_x,
        grad_proj_y,
        small[:tap_count],
        small[tap_count],
        wide[:block_width],
        small[tap_count + 1],
        wide[block_width:],
        small[tap_count + 2],
        small[tap_count + 3],
        grad_proj_out,
        gains[1],
        grad_mlp_gate,
        grad_mlp_up,
        grad_mlp_down,
    )


def solution(mesh):
    placed = (
        P("dp", None),
        P("dp"),
        P(),
        P(None, "tensor"),
        P(None, "tensor"),
        P(None, "tensor"),
        P("tensor"),
        P(None, "tensor"),
        P("tensor"),
        P(None, "tensor"),
        P("tensor"),
        P("tensor"),
        P("tensor", None),
        P(),
        P("dp", "tensor"),
        P("dp", "tensor"),
        P("dp", "tensor"),
        P("dp", None),
    )
    return jax.shard_map(
        inner,
        mesh=mesh,
        in_specs=placed,
        out_specs=(
            P(("dp", "tensor"), None),
            P(("dp", "tensor"), None),
            P(),
            P("dp", "tensor"),
            P("dp", "tensor"),
            P(None, "tensor"),
            P("tensor"),
            P(None, "tensor"),
            P("tensor"),
            P(None, "tensor"),
            P("tensor"),
            P("tensor"),
            P("tensor", "dp"),
            P(),
            P("dp", "tensor"),
            P("dp", "tensor"),
            P("dp", "tensor"),
        ),
        check_vma=False,
    )
```

profile of v0, /device:TPU:0, one launch (start us, length us, event | category | flops | bytes accessed | tf_op | source)
XLA Modules:
  0.0 763.6 jit_solution(14793124145100367484)
XLA Ops:
  7.2 1.7 slice.87
  8.9 5.5 collective-permute-start
  18.4 1.6 collective-permute-start.2
  25.4 2.3 fusion
  28.4 1.9 constant_dynamic-slice_fusion.4
  31.3 1.9 copy.90
  34.5 4.0 fusion.2
  38.6 1.6 collective-permute-start.6
  41.3 1.5 fusion.56
  46.8 4.9 convolution_convert_fusion.8
  55.0 2.1 copy.91
  57.0 1.6 constant_dynamic-slice_fusion.5
  58.7 2.3 fusion.88
  62.3 2.6 copy.137
  64.8 2.5 copy.136
  70.4 5.8 convert_multiply_fusion.3
  76.3 5.3 collective-permute-done.7.refs_3_
  81.6 1.7 place.3
  86.2 2.1 constant_dynamic-slice_fusion.3.tok_ref
  88.3 2.0 constant_dynamic-slice_fusion.2.cot_ref
  90.3 14.2 %scan.1 = (f32[512,640]{1,0:T(8,128)S(1)}, f32[1,640]{1,0:T(1,128)S(1)}) custom-call(f32[512,640]{1,0:T(8,128)S(1)} %copy-done.1, f32[512,640]{1,0:T(8,128)S(1)} %copy-done.12), custom_call_target="tpu_custom_call" | custom-call | tf_op jit(solution)/shard_map/scan/pallas_call | solution.py:846
  104.5 5.7 multiply_convert_fusion
  110.2 3.7 convolution_convert_fusion.7
  116.2 1.7 copy-done.14
  117.9 108.7 %middle.1 = (f32[128,2560]{1,0:T(8,128)S(1)}, bf16[2,2,2,2,128,2560]{5,4,3,2,1,0:T(8,128)(2,1)S(1)}, bf16[2,2,2,2,128,2560]{5,4,3,2,1,0:T(8,128)(2,1)}) custom-call(bf16[2,2,128,2560]{3,2,1,0:T(8,128)(2,1)S(1)} %bitcast.108, bf16[128,2560]{1,0:T(8,128)(2,1)S(1)} %copy-done.7, bf16[128,2560]{1,0:T(8,128)(2,1)S(1)} %copy-done.5, f32[1,2560]{1,0:T(1,128)S(1)} %reshape.203.gain_ref), custom_call_target="tpu_custom_call" | custom-call | tf_op jit(solution)/shard_map/middle/pallas_call | solution.py:409
  227.7 4.0 copy-done.35
  231.7 10.4 %fusion.89 = f32[2048,512]{1,0:T(8,128)} fusion(bf16[2048,2560]{1,0:T(8,128)(2,1)} %bitcast.111, bf16[2560,512]{1,0:T(8,128)(2,1)} %bitcast.153), kind=kOutput, calls=%fused_computation.178 | convolution fusion | flops 5368709120 | bytes 17301504 | tf_op jit(solution)/shard_map/dot_general | solution.py:45
  242.1 10.4 %fusion.90 = f32[2048,512]{1,0:T(8,128)} fusion(bf16[2048,2560]{1,0:T(8,128)(2,1)} %bitcast.112, bf16[2560,512]{1,0:T(8,128)(2,1)} %bitcast.155), kind=kOutput, calls=%fused_computation.179 | convolution fusion | flops 5368709120 | bytes 17301504 | tf_op jit(solution)/shard_map/dot_general | solution.py:45
  252.4 1.5 all-gather.8.cloned.1.call-done
  253.9 15.6 %select_convert_fusion = (bf16[2048,512]{1,0:T(8,128)(2,1)}, bf16[2048,512]{1,0:T(8,128)(2,1)}, bf16[2048,512]{1,0:T(8,128)(2,1)S(1)}) fusion(pred[512]{0:T(512)(128)(4,1)S(1)} %iota_compare_fusion, f32[2048,512]{1,0:T(8,128)} %fusion.89, f32[2048,512]{1,0:T(8,128)} %fusion.90, bf16[2048,2560]{1,0:T(8,128)(2,1)} %bitcast.151, bf16[2560,512]{1,0:T(8,128)(2,1)} %bitcast.157), kind=kOutput, calls=%fused_computation.25 | convolution fusion | flops 5399117824 | bytes 27787776 | tf_op jit(solution)/shard_map/dot_general | solution.py:45
  270.8 8.3 %convolution_convert_fusion = bf16[2048,2560]{1,0:T(8,128)(2,1)} fusion(bf16[2048,512]{1,0:T(8,128)(2,1)S(1)} %get-tuple-element.101, bf16[2560,512]{1,0:T(8,128)(2,1)S(1)} %bitcast.158), kind=kOutput, calls=%fused_computation.1 | convolution fusion | flops 5373952000 | bytes 15204352 | tf_op jit(solution)/shard_map/dot_general | solution.py:33
  279.1 10.0 %convolution_convert_fusion.5 = bf16[2560,512]{1,0:T(8,128)(2,1)} fusion(bf16[2048,2560]{1,0:T(8,128)(2,1)} %bitcast.113, bf16[2048,512]{1,0:T(8,128)(2,1)} %get-tuple-element.99), kind=kOutput, calls=%fused_computation.14 | convolution fusion | flops 5370019840 | bytes 15204352 | tf_op jit(solution)/shard_map/dot_general | solution.py:39
  289.6 10.1 %convolution_convert_fusion.4 = bf16[2560,512]{1,0:T(8,128)(2,1)} fusion(bf16[2048,2560]{1,0:T(8,128)(2,1)} %bitcast.114, bf16[2048,512]{1,0:T(8,128)(2,1)} %get-tuple-element.100), kind=kOutput, calls=%fused_computation.13 | convolution fusion | flops 5370019840 | bytes 15204352 | tf_op jit(solution)/shard_map/dot_general | solution.py:39
  299.8 12.2 %fusion.91 = f32[2048,2560]{1,0:T(8,128)} fusion(bf16[2048,512]{1,0:T(8,128)(2,1)} %get-tuple-element.99, bf16[2560,512]{1,0:T(8,128)(2,1)} %bitcast.154), kind=kOutput, calls=%fused_computation.180 | convolution fusion | flops 5368709120 | bytes 25690112 | tf_op jit(solution)/shard_map/dot_general | solution.py:33
  312.0 11.1 %convolution_convert_fusion.6 = bf16[2560,512]{1,0:T(8,128)(2,1)} fusion(bf16[2048,2560]{1,0:T(8,128)(2,1)} %bitcast.152, bf16[2048,512]{1,0:T(8,128)(2,1)S(1)} %copy-done.107), kind=kOutput, calls=%fused_computation.15 | convolution fusion | flops 5370019840 | bytes 15204352 | tf_op jit(solution)/shard_map/dot_general | solution.py:39
  323.1 13.1 %add_convert_fusion = bf16[2048,2560]{1,0:T(8,128)(2,1)} fusion(f32[2048,2560]{1,0:T(8,128)} %fusion.91, bf16[2048,512]{1,0:T(8,128)(2,1)} %get-tuple-element.100, bf16[2560,512]{1,0:T(8,128)(2,1)S(1)} %bitcast.156), kind=kOutput, calls=%fused_computation | convolution fusion | flops 5379194880 | bytes 36175872 | tf_op jit(solution)/shard_map/dot_general | solution.py:33
  339.5 77.9 %back.1 = (f32[128,2560]{1,0:T(8,128)S(1)}, bf16[2,2,128,2560]{3,2,1,0:T(8,128)(2,1)S(1)}, f32[1,2560]{1,0:T(1,128)S(1)}) custom-call(bf16[2,2,2,2,128,2560]{5,4,3,2,1,0:T(8,128)(2,1)} %bitcast.121, f32[128,2560]{1,0:T(8,128)S(1)} %copy-done.10, bf16[128,2560]{1,0:T(8,128)(2,1)S(1)} %copy-done.6, f32[1,2560]{1,0:T(1,128)S(1)} %reshape.203.gain_ref), custom_call_target="tpu_custom_call" | custom-call | tf_op jit(solution)/shard_map/back/pallas_call | solution.py:552
  417.4 2.9 fusion.19
  420.3 16.1 %scan_back.1 = (f32[512,640]{1,0:T(8,128)S(1)}, f32[1,640]{1,0:T(1,128)}) custom-call(f32[512,640]{1,0:T(8,128)S(1)} %copy-done.2, f32[512,640]{1,0:T(8,128)S(1)} %get-tuple-element.154.refs_1_), custom_call_target="tpu_custom_call" | custom-call | tf_op jit(solution)/shard_map/scan_back/pallas_call | solution.py:846
  436.4 2.2 convolution_convert_fusion.2
  442.2 2.3 convolution_convert_fusion.3
  448.0 4.1 multiply_reduce_fusion
  454.3 2.1 copy.104
  456.4 2.2 fusion.95
  458.6 1.8 copy.116
  460.4 8.0 %fusion.83 = (bf16[640]{0:T(1024)(128)(2,1)S(1)}, bf16[512,640]{1,0:T(8,128)(2,1)S(1)}) fusion(f32[640]{0:T(1024)S(1)} %copy-done.89, f32[512,512]{1,0:T(8,128)} %copy.137, f32[512,128]{1,0:T(8,128)} %copy-done.51, f32[512,640]{1,0:T(8,128)} %copy-done.3, f32[640]{0:T(1024)S(1)} %copy-done.82, f32[640]{0:T(1024)S(1)} %copy-done.81, f32[512,512]{1,0:T(8,128)} %copy.136, ...), kind=kLoop, calls=%fused_computation.174 | loop fusion | flops 12451200 | bytes 9858817 | tf_op jit(solution)/shard_map/reduce_sum | solution.py:1146
  470.0 2.0 copy.101
  472.1 2.2 fusion.94
  474.3 1.8 copy.111
  481.1 2.5 copy.138
  487.0 1.4 fusion.50
  488.7 6.6 fusion.93
  497.3 3.9 multiply_reduce_fusion.4
  503.0 1.8 multiply_multiply_fusion.7
  507.2 25.9 %collective-permute-done.9 = bf16[2,2,320,640]{3,2,1,0:T(8,128)(2,1)} collective-permute-done((bf16[2,2,320,640]{3,2,1,0:T(8,128)(2,1)}, bf16[2,2,320,640]{3,2,1,0:T(8,128)(2,1)}, u32[]{:S(2)}, u32[]{:S(2)}) %collective-permute-start.9) | collective-permute-done | bytes 1638432 | tf_op jit(solution)/shard_map/ppermute | solution.py:55
  533.1 3.1 collective-permute-done.10
  537.5 3.0 fusion.11.o_ref
  540.5 3.2 fusion.12.y_ref
  543.7 4.0 convolution_convert_fusion.1
  547.8 3.7 add_convert_fusion.1
  553.7 161.7 %last.1 = (f32[128,2560]{1,0:T(8,128)S(1)}, f32[1,2560]{1,0:T(1,128)S(1)}, f32[320,640]{1,0:T(8,128)S(1)}, bf16[80,640]{1,0:T(8,128)(2,1)S(1)}, f32[320,640]{1,0...) custom-call(bf16[2,2,128,2560]{3,2,1,0:T(8,128)(2,1)} %bitcast.138, ...), custom_call_target="tpu_custom_call" | custom-call | tf_op jit(solution)/shard_map/last/pallas_call | solution.py:726
  716.4 22.1 %final.1 = (bf16[8,80,640]{2,1,0:T(8,128)(2,1)S(1)}, f32[2,2560]{1,0:T(2,128)S(1)}) custom-call(bf16[80,640]{1,0:T(8,128)(2,1)S(1)} %get-tuple-element.118.small_ref, f32[1,2560]{1,0:T(1,128)S(1)} %get-tuple-element.119.gain1_ref, f32[1,2560]{1,0:T(1,128)S(1)} %get-tuple-element.120.gain2_ref), custom_call_target="tpu_custom_call" | custom-call | tf_op jit(solution)/shard_map/final/pallas_call | solution.py:293
  741.7 2.8 convert_add_fusion.2
  749.9 1.4 copy.152
  (320 shorter events, 79.7 us)
Async XLA Ops:
  7.2 103.0 %copy-start = (bf16[640,2560]{1,0:T(8,128)(2,1)S(1)}, bf16[640,2560]{1,0:T(8,128)(2,1)}, u32[]{:S(2)}) copy-start(bf16[640,2560]{1,0:T(8,128)(2,1)} %param.30) | copy-start | bytes 9830404
  7.2 224.5 %all-gather.4.cloned.1.call-start = ((), (), s32[]{:S(2)}) async-start(), calls=%async_computation.4 | async-start | bytes 3932160 | tf_op jit(solution)/shard_map/all_gather | solution.py:949
  8.9 29.6 %collective-permute-start = (bf16[16,2560]{1,0:T(8,128)(2,1)}, bf16[16,2560]{1,0:T(8,128)(2,1)}, u32[]{:S(2)}, u32[]{:S(2)}) collective-permute-start(bf16[16,2560]{1,0:T(8,128)(2,1)} %slice.87), channel_id=1, source_target_pairs={{0,4},{4,8},{8,12},{12,16},{16,20},{20,24},{24,28},{1,5},{5,9},{9,... | collective-permute-start | bytes 245768 | tf_op jit(solution)/shard_map/ppermute | solution.py:51
  15.7 5.2 copy-start.23
  17.4 26.0 %collective-permute-start.1 = (bf16[1,320,512]{2,1,0:T(8,128)(2,1)}, bf16[1,320,512]{2,1,0:T(8,128)(2,1)}, u32[]{:S(2)}, u32[]{:S(2)}) collective-permute-start(bf16[1,320,512]{2,1,0:T(8,128)(2,1)} %get-tuple-element.74), channel_id=1, source_target_pairs={{0,4},{4,0},{8,12},{12,8},{16,20},{20,16},{24,28},{28,24},{1,5},{5... | collective-permute-start | bytes 983048 | tf_op jit(solution)/shard_map/ppermute | solution.py:55
  18.4 26.0 %collective-permute-start.2 = (bf16[1,320,512]{2,1,0:T(8,128)(2,1)}, bf16[1,320,512]{2,1,0:T(8,128)(2,1)}, u32[]{:S(2)}, u32[]{:S(2)}) collective-permute-start(bf16[1,320,512]{2,1,0:T(8,128)(2,1)} %get-tuple-element.75), channel_id=1, source_target_pairs={{0,8},{4,12},{8,0},{12,4},{16,24},{20,28},{24,16},{28,20},{1,9},{5... | collective-permute-start | bytes 983048 | tf_op jit(solution)/shard_map/ppermute | solution.py:55
  19.9 24.4 %collective-permute-start.3 = (bf16[1,320,512]{2,1,0:T(8,128)(2,1)}, bf16[1,320,512]{2,1,0:T(8,128)(2,1)}, u32[]{:S(2)}, u32[]{:S(2)}) collective-permute-start(bf16[1,320,512]{2,1,0:T(8,128)(2,1)} %get-tuple-element.76), channel_id=1, source_target_pairs={{0,12},{4,8},{8,4},{12,0},{16,28},{20,24},{24,20},{28,16},{1,13},{... | collective-permute-start | bytes 983048 | tf_op jit(solution)/shard_map/ppermute | solution.py:55
  24.4 51.8 %collective-permute-start.5 = (bf16[2,320,512]{2,1,0:T(8,128)(2,1)}, bf16[2,320,512]{2,1,0:T(8,128)(2,1)}, u32[]{:S(2)}, u32[]{:S(2)}) collective-permute-start(bf16[2,320,512]{2,1,0:T(8,128)(2,1)} %get-tuple-element.79), channel_id=1, source_target_pairs={{0,4},{4,0},{8,12},{12,8},{16,20},{20,16},{24,28},{28,24},{1,5},{5... | collective-permute-start | bytes 1966088 | tf_op jit(solution)/shard_map/ppermute | solution.py:55
  27.7 6.8 copy-start.78
  31.3 27.4 %copy-start.72 = (bf16[256,512]{0,1:T(8,128)(2,1)}, bf16[256,512]{0,1:T(8,128)(2,1)S(1)}, u32[]{:S(2)}) copy-start(bf16[256,512]{0,1:T(8,128)(2,1)S(1)} %copy.96) | copy-start | bytes 786436
  34.5 4.0 copy-start.98
  34.5 6.7 copy-start.56
  34.5 6.7 copy-start.79
  38.6 37.7 %collective-permute-start.6 = (bf16[2,320,512]{2,1,0:T(8,128)(2,1)}, bf16[2,320,512]{2,1,0:T(8,128)(2,1)}, u32[]{:S(2)}, u32[]{:S(2)}) collective-permute-start(bf16[2,320,512]{2,1,0:T(8,128)(2,1)} %get-tuple-element.80), channel_id=1, source_target_pairs={{0,8},{4,12},{8,0},{12,4},{16,24},{20,28},{24,16},{28,20},{1,9},{5... | collective-permute-start | bytes 1966088 | tf_op jit(solution)/shard_map/ppermute | solution.py:55
  43.4 38.2 %collective-permute-start.7 = (bf16[2,320,512]{2,1,0:T(8,128)(2,1)}, bf16[2,320,512]{2,1,0:T(8,128)(2,1)}, u32[]{:S(2)}, u32[]{:S(2)}) collective-permute-start(bf16[2,320,512]{2,1,0:T(8,128)(2,1)} %get-tuple-element.81), channel_id=1, source_target_pairs={{0,12},{4,8},{8,4},{12,0},{16,28},{20,24},{24,20},{28,16},{1,13},{... | collective-permute-start | bytes 1966088 | tf_op jit(solution)/shard_map/ppermute | solution.py:55
  46.8 195.3 %all-gather.6.cloned.1.call-start = ((), (), s32[]{:S(2)}) async-start(), calls=%async_computation.5 | async-start | bytes 3932160 | tf_op jit(solution)/shard_map/all_gather | solution.py:949
  46.8 4.9 copy-start.93
  57.0 4.0 copy-start.44
  57.0 4.0 copy-start.74
  58.7 8.8 %collective-permute-start.4 = (bf16[512,128]{1,0:T(8,128)(2,1)}, bf16[512,128]{1,0:T(8,128)(2,1)}, u32[]{:S(2)}, u32[]{:S(2)}) collective-permute-start(bf16[512,128]{1,0:T(8,128)(2,1)} %constant_dynamic-slice_fusion.5), channel_id=1, source_target_pairs={{0,1},{1,0},{2,3},{3,2},{4,5},{5,4},{6,7},{7,6},{8,9},{9,8},{10,11... | collective-permute-start | bytes 393224 | tf_op jit(solution)/shard_map/ppermute | solution.py:55
  68.9 7.4 copy-start.45
  70.3 6.0 copy-start.51
  70.4 11.2 %copy-start.32 = (bf16[2,320,512]{2,1,0:T(8,128)(2,1)S(1)}, bf16[2,320,512]{2,1,0:T(8,128)(2,1)}, u32[]{:S(2)}) copy-start(bf16[2,320,512]{2,1,0:T(8,128)(2,1)} %copy-done.31) | copy-start | bytes 1966084
  85.4 168.5 %all-gather.8.cloned.1.call-start = ((), (), s32[]{:S(2)}) async-start(), calls=%async_computation.6 | async-start | bytes 3932160 | tf_op jit(solution)/shard_map/all_gather | solution.py:949
  86.1 4.1 copy-start.1
  86.1 4.1 copy-start.12
  90.3 14.2 %copy-start.64 = (bf16[512,2560]{1,0:T(8,128)(2,1)S(1)}, bf16[512,2560]{1,0:T(8,128)(2,1)}, u32[]{:S(2)}) copy-start(bf16[512,2560]{1,0:T(8,128)(2,1)} %fusion.2) | copy-start | bytes 7864324
  104.4 5.7 copy-start.20
  113.9 437.5 %reduce-scatter.9.cloned.1.call-start = ((), (), s32[]{:S(2)}) async-start(), calls=%async_computation.9 | async-start | bytes 3932160 | tf_op jit(solution)/shard_map/reduce_scatter | solution.py:956
  227.7 4.0 copy-start.35
  253.9 16.9 %copy-start.100 = (bf16[8,320,512]{2,1,0:T(8,128)(2,1)S(1)}, bf16[8,320,512]{2,1,0:T(8,128)(2,1)}, u32[]{:S(2)}) copy-start(bf16[8,320,512]{2,1,0:T(8,128)(2,1)} %all-gather.8.cloned.1.call-done) | copy-start | bytes 7864324
  289.2 262.3 %reduce-scatter.11.cloned.1.call-start = ((), (), s32[]{:S(2)}) async-start(), calls=%async_computation.10 | async-start | bytes 3932160 | tf_op jit(solution)/shard_map/reduce_scatter | solution.py:956
  299.8 251.7 %reduce-scatter.7.cloned.1.call-start = ((), (), s32[]{:S(2)}) async-start(), calls=%async_computation.8 | async-start | bytes 3932160 | tf_op jit(solution)/shard_map/reduce_scatter | solution.py:956
  299.8 12.2 %copy-start.107 = (bf16[2048,512]{1,0:T(8,128)(2,1)S(1)}, bf16[2048,512]{1,0:T(8,128)(2,1)}, u32[]{:S(2)}) copy-start(bf16[2048,512]{1,0:T(8,128)(2,1)} %copy-done.106) | copy-start | bytes 6291460
  312.0 11.1 %copy-start.99 = (bf16[8,320,512]{2,1,0:T(8,128)(2,1)S(1)}, bf16[8,320,512]{2,1,0:T(8,128)(2,1)}, u32[]{:S(2)}) copy-start(bf16[8,320,512]{2,1,0:T(8,128)(2,1)} %all-gather.6.cloned.1.call-done) | copy-start | bytes 7864324
  336.2 405.5 %reduce-scatter.5.cloned.1.call-start = ((), (), s32[]{:S(2)}) async-start(), calls=%async_computation.7 | async-start | bytes 11141120 | tf_op jit(solution)/shard_map/reduce_scatter | solution.py:1071
  339.5 77.9 %copy-start.21 = (f32[512,640]{1,0:T(8,128)S(1)}, f32[512,640]{1,0:T(8,128)}, u32[]{:S(2)}) copy-start(f32[512,640]{1,0:T(8,128)} %copy-done.20) | copy-start | bytes 3932164
  339.5 77.9 %copy-start.103 = (f32[512,640]{1,0:T(8,128)S(1)}, f32[512,640]{1,0:T(8,128)}, u32[]{:S(2)}) copy-start(f32[512,640]{1,0:T(8,128)} %get-tuple-element.170) | copy-start | bytes 3932164
  420.3 19.7 %copy-start.101 = (bf16[512,640]{1,0:T(8,128)(2,1)}, bf16[512,640]{1,0:T(8,128)(2,1)S(1)}, u32[]{:S(2)}) copy-start(bf16[512,640]{1,0:T(8,128)(2,1)S(1)} %get-tuple-element.106) | copy-start | bytes 1966084
  420.3 16.1 %copy-start.105 = (bf16[512,640]{1,0:T(8,128)(2,1)S(1)}, bf16[512,640]{1,0:T(8,128)(2,1)}, u32[]{:S(2)}) copy-start(bf16[512,640]{1,0:T(8,128)(2,1)} %copy-done.104) | copy-start | bytes 1966084
  436.4 10.6 %copy-start.3 = (f32[512,640]{1,0:T(8,128)}, f32[512,640]{1,0:T(8,128)S(1)}, u32[]{:S(2)}) copy-start(f32[512,640]{1,0:T(8,128)S(1)} %get-tuple-element.108) | copy-start | bytes 3932164
  442.2 4.8 copy-start.42
  448.0 4.1 copy-start.95
  479.3 17.0 %collective-permute-start.8 = (bf16[512,128]{1,0:T(8,128)(2,1)}, bf16[512,128]{1,0:T(8,128)(2,1)S(1)}, u32[]{:S(2)}, u32[]{:S(2)}) collective-permute-start(bf16[512,128]{1,0:T(8,128)(2,1)} %select_convert_fusion.2), channel_id=1, source_target_pairs={{0,1},{1,0},{2,3},{3,2},{4,5},{5,4},{6,7},{7,6},{8,9},{9,8},{10,11... | collective-permute-start | bytes 393224 | tf_op jit(solution)/shard_map/ppermute | solution.py:55
  483.7 4.8 copy-start.76
  483.7 4.9 copy-start.102
  483.7 49.4 %collective-permute-start.9 = (bf16[2,2,320,640]{3,2,1,0:T(8,128)(2,1)}, bf16[2,2,320,640]{3,2,1,0:T(8,128)(2,1)}, u32[]{:S(2)}, u32[]{:S(2)}) collective-permute-start(bf16[2,2,320,640]{3,2,1,0:T(8,128)(2,1)} %dynamic-slice_bitcast_fusion.1), channel_id=1, source_target_pairs={{0,4},{4,0},{8,12},{12,8},{16,20},{20,16},{24,28},{28,24},{1,5},{5... | collective-permute-start | bytes 4915208 | tf_op jit(solution)/shard_map/ppermute | solution.py:55
  485.1 51.1 %collective-permute-start.10 = (bf16[2,2,320,640]{3,2,1,0:T(8,128)(2,1)}, bf16[2,2,320,640]{3,2,1,0:T(8,128)(2,1)}, u32[]{:S(2)}, u32[]{:S(2)}) collective-permute-start(bf16[2,2,320,640]{3,2,1,0:T(8,128)(2,1)} %dynamic-slice_bitcast_fusion), channel_id=1, source_target_pairs={{0,8},{4,12},{8,0},{12,4},{16,24},{20,28},{24,16},{28,20},{1,9},{5... | collective-permute-start | bytes 4915208 | tf_op jit(solution)/shard_map/ppermute | solution.py:55
  488.6 6.7 copy-start.77
  488.6 7.7 %copy-start.55 = (f32[512,256]{1,0:T(8,128)S(1)}, f32[512,256]{1,0:T(8,128)}, u32[]{:S(2)}) copy-start(f32[512,256]{1,0:T(8,128)} %copy-done.54) | copy-start | bytes 1572868
  488.6 7.7 %copy-start.41 = (f32[512,512]{1,0:T(8,128)S(1)}, f32[512,512]{1,0:T(8,128)}, u32[]{:S(2)}) copy-start(f32[512,512]{1,0:T(8,128)} %copy.136) | copy-start | bytes 3145732
  488.6 7.7 %copy-start.43 = (f32[512,512]{1,0:T(8,128)S(1)}, f32[512,512]{1,0:T(8,128)}, u32[]{:S(2)}) copy-start(f32[512,512]{1,0:T(8,128)} %copy.137) | copy-start | bytes 3145732
  488.6 7.7 %copy-start.47 = (f32[512,128]{1,0:T(8,128)S(1)}, f32[512,128]{1,0:T(8,128)}, u32[]{:S(2)}) copy-start(f32[512,128]{1,0:T(8,128)} %copy-done.45) | copy-start | bytes 786436
  488.6 7.7 %copy-start.50 = (f32[512,512]{1,0:T(8,128)S(1)}, f32[512,512]{1,0:T(8,128)}, u32[]{:S(2)}) copy-start(f32[512,512]{1,0:T(8,128)} %copy.138) | copy-start | bytes 3145732
  488.7 7.7 %copy-start.53 = (f32[512,128]{1,0:T(8,128)S(1)}, f32[512,128]{1,0:T(8,128)}, u32[]{:S(2)}) copy-start(f32[512,128]{1,0:T(8,128)} %copy-done.51) | copy-start | bytes 786436
  506.8 30.7 %copy-start.59 = (bf16[2560,640]{1,0:T(8,128)(2,1)S(1)}, bf16[2560,640]{1,0:T(8,128)(2,1)}, u32[]{:S(2)}) copy-start(bf16[2560,640]{1,0:T(8,128)(2,1)} %copy-done.58) | copy-start | bytes 9830404
  507.2 33.4 %copy-start.61 = (bf16[2560,640]{1,0:T(8,128)(2,1)S(1)}, bf16[2560,640]{1,0:T(8,128)(2,1)}, u32[]{:S(2)}) copy-start(bf16[2560,640]{1,0:T(8,128)(2,1)} %copy-done.60) | copy-start | bytes 9830404
  536.2 7.5 collective-permute-start.11
  540.5 7.2 slice-start
  543.7 4.0 copy-start.57
  543.7 4.0 slice-start.1
  716.4 24.1 %copy-start.17 = (f32[128,2560]{1,0:T(8,128)}, f32[128,2560]{1,0:T(8,128)S(1)}, u32[]{:S(2)}) copy-start(f32[128,2560]{1,0:T(8,128)S(1)} %get-tuple-element.193) | copy-start | bytes 3932164
  716.4 24.1 %copy-start.25 = (f32[320,640]{1,0:T(8,128)}, f32[320,640]{1,0:T(8,128)S(1)}, u32[]{:S(2)}) copy-start(f32[320,640]{1,0:T(8,128)S(1)} %get-tuple-element.125) | copy-start | bytes 2457604
  716.4 24.2 %copy-start.27 = (f32[320,640]{1,0:T(8,128)}, f32[320,640]{1,0:T(8,128)S(1)}, u32[]{:S(2)}) copy-start(f32[320,640]{1,0:T(8,128)S(1)} %get-tuple-element.196) | copy-start | bytes 2457604
  (65 other events, 127.3 us)
Sparse Core Ops, SparseCore 0:
  46.9 68.6 all-gather.3
  117.6 67.0 all-gather.5
  186.8 67.0 all-gather.7
  289.3 65.7 reduce-scatter.8
  357.2 65.6 reduce-scatter.10
  425.0 65.7 reduce-scatter.6
  493.2 153.2 reduce-scatter.4
where the time goes:
time: 773 us; the launch traced here: 764 us
  Pallas kernels  406 us (53%)
  matrix products  156 us (20%)
  local copies, waits for them, and re-layouts  85.7 us (11%)
  other arithmetic  46.5 us (6%)
  waiting for transfers between devices  36.7 us (5%)
  starting transfers between devices  16.6 us (2%)
  between operations  15.7 us (2%)
    pallas_call x1, Pallas kernels, last_pass(): pl.pallas_call(functools.partial(last_kernel, plan), name='last', out_sha...  162 us
    pallas_call x1, Pallas kernels, middle(): pl.pallas_call(middle_kernel, name='middle', out_shape=(jax.ShapeDtypeStr...  109 us
    pallas_call x1, Pallas kernels, back_pass(): pl.pallas_call(back_kernel, name='back', out_shape=(jax.ShapeDtypeStruct(...  77.9 us
    dot_general x9, matrix products, matmul(): return jnp.dot(left_rows, right_rows, preferred_element_type=jnp.float32)  55 us
    dot_general x8, matrix products, contract_last(): lax.dot_general(left_rows, right_rows, (((1,), (1,)), ((), ())), preferre...  49.1 us
    unnamed x227, local copies, waits for them, and re-layouts  45.5 us
    dot_general x8, matrix products, contract_first(): lax.dot_general(left_rows, right_rows, (((0,), (0,)), ((), ())), preferre...  42.7 us
    ppermute x10, waiting for transfers between devices, flipped(): lax.ppermute(array, axis, [(i, i ^ mask) for i in range(lax.axis_size(axi...  34.4 us
  transfers between devices with their start and end apart: 19, of which 4 were waited for; matrix products, arithmetic and copies ran while one was open for 27% of the time, Pallas kernels for 53%

commit v1 on v0

--- a/solution.py
+++ b/solution.py
@@ -209,6 +209,54 @@
     )(*pieces)
 
 
+def pick_kernel(count, *refs):
+    for spot, out in zip(spots_of_four(), refs[count:]):
+        for i in range(count):
+            out[i] = refs[i][spot]
+
+
+def picked(*parts):
+    _, rows, share = parts[0].shape
+    return pl.pallas_call(
+        functools.partial(pick_kernel, len(parts)),
+        name="pick",
+        out_shape=[jax.ShapeDtypeStruct((len(parts), rows, share), jnp.bfloat16)] * GROUP,
+        compiler_params=pltpu.CompilerParams(vmem_limit_bytes=24 * 2**20),
+    )(*parts)
+
+
+def join_kernel(count, *refs):
+    pieces, outs, slots = refs[:GROUP], refs[GROUP : GROUP + count], refs[GROUP + count]
+    for spot, piece in zip(spots_of_four(), pieces):
+        for i in range(count):
+            slots[i, spot] = piece[i]
+    rows, width = outs[0].shape
+    share, over = share_width(width), overlap_of(width)
+
+    def strip(step, carry):
+        at = pl.ds(pl.multiple_of(step * STRIP, STRIP), STRIP)
+        for i in range(count):
+            for place in range(GROUP):
+                skip = over * (place // (GROUP - 1))
+                outs[i][at, share * place : min(share * (place + 1), width)] = slots[
+                    i, place, at, skip:share
+                ].astype(jnp.float32)
+        return carry
+
+    lax.fori_loop(0, rows // STRIP, strip, 0)
+
+
+def joined(pieces, width):
+    count, rows, share = pieces[0].shape
+    return pl.pallas_call(
+        functools.partial(join_kernel, count),
+        name="join",
+        out_shape=[jax.ShapeDtypeStruct((rows, width), jnp.float32)] * count,
+        scratch_shapes=[pltpu.VMEM((count, GROUP, rows, share), jnp.bfloat16)],
+        compiler_params=pltpu.CompilerParams(vmem_limit_bytes=32 * 2**20),
+    )(*pieces)
+
+
 class Collect:
     def __init__(self, part_ref, out_ref, slots, send_sem, recv_sem, own_sem):
         spot, *spots = spots_of_four()
@@ -429,6 +477,37 @@
             collective_id=1, has_side_effects=True, vmem_limit_bytes=32 * 2**20
         ),
     )(part.reshape(2, 2, rows, width), tok, cot, gain.reshape(1, width))
+
+
+def product_pair_kernel(left1_ref, left2_ref, right1_ref, right2_ref, out_ref):
+    tile = 512
+    for at in range(0, out_ref.shape[1], tile):
+        part = slice(at, at + tile)
+        total = contract_last(left1_ref[...], right1_ref[part])
+        total += contract_last(left2_ref[...], right2_ref[part])
+        out_ref[:, part] = total.astype(out_ref.dtype)
+
+
+def product_pair(left1, left2, right1, right2):
+    rows, depth = left1.shape
+    width = right1.shape[0]
+    block = 256
+    left = pl.BlockSpec((block, depth), lambda i: (i, 0))
+    right = pl.BlockSpec((width, depth), lambda i: (0, 0))
+    return pl.pallas_call(
+        product_pair_kernel,
+        name="product_pair",
+        grid=(rows // block,),
+        out_shape=jax.ShapeDtypeStruct((rows, width), jnp.bfloat16),
+        in_specs=[left, left, right, right],
+        out_specs=pl.BlockSpec((block, width), lambda i: (i, 0)),
+        cost_estimate=pl.CostEstimate(
+            flops=4 * rows * depth * width,
+            bytes_accessed=2 * (2 * rows * depth + 2 * width * depth + rows * width),
+            transcendentals=0,
+        ),
+        compiler_params=pltpu.CompilerParams(vmem_limit_bytes=32 * 2**20),
+    )(left1, left2, right1, right2)
 
 
 def norm_back(rows, back, base_ref, gain_ref, keep_ref, gain_acc):
@@ -653,7 +732,7 @@
 
 
 def last_plan(bits, rows, few_rows, width):
-    wide = width // 128 * 4 // 5 * 128
+    wide = -(-width // 256) * 128
     swapped = [1, 0, *range(2, bits)]
     return [
         (list(range(bits)), 0, halve_scratch(bits, rows + few_rows, wide)),
@@ -665,8 +744,8 @@
 
 def last_kernel(
     plan, part_ref, tok_ref, keep_ref, gain_ref, wide_ref, few_ref, y_ref, o_ref,
-    row1_ref, row2_ref, row3_ref,
-    grad_ref, gain_out, wide_out, few_out, y_out, o_out, row1_out, row2_out, row3_out,
+    row_ref,
+    grad_ref, gain_out, wide_out, few_out, y_out, o_out, row_out,
     q, core_buf, link_buf, gain_acc, *refs
 ):
     sum_sems, refs = refs[:3], refs[3:]
@@ -682,10 +761,10 @@
     both = {"dp": lax.axis_index("dp") + (spots[2] - spot) * (1 << FIRST_BIT)}
     greet([across(*LINKS[2]), across(*CORE), both] + peers)
     total = SumTensor(part_ref, q, core_buf, link_buf, *sum_sems)
-    for each in halvings:
+    turns = [halvings[i] for i in (2, 3, 1, 0)]
+    for each in turns:
         each.start(0)
-    rows = zip((row1_ref, row2_ref, row3_ref), (row1_out, row2_out, row3_out))
-    collects = [Collect(part, out, *refs[4 * i : 4 * i + 4]) for i, (part, out) in enumerate(rows)]
+    collects = [Collect(row_ref, row_out, *refs)]
     total.pass_on()
     gain_acc[...] = jnp.zeros_like(gain_acc)
 
@@ -699,7 +778,7 @@
     lax.fori_loop(0, tok_ref.shape[0] // STRIP, strip, 0)
     gain_out[...] = jnp.sum(gain_acc[...], axis=0, keepdims=True)
     for step in range(bits):
-        for each in halvings:
+        for each in turns:
             if step < len(each.order):
                 each.land(step)
     rows = wide_out.shape[0]
@@ -716,7 +795,7 @@
         each.finish()
 
 
-def last_pass(part, tok, keep, gain, wide, few, side_y, side_o, parts, hidden_width):
+def last_pass(part, tok, keep, gain, wide, few, side_y, side_o, rows_part, hidden_width):
     rows, width = tok.shape
     vmem, anywhere = pl.BlockSpec(memory_space=pltpu.VMEM), pl.BlockSpec(memory_space=pl.ANY)
     bits = wide.shape[0].bit_length() - 1
@@ -733,10 +812,10 @@
             jax.ShapeDtypeStruct(few.shape[1:], jnp.bfloat16),
             block,
             block,
-            *[jax.ShapeDtypeStruct((parts[0].shape[1], hidden_width), jnp.float32)] * 3,
+            jax.ShapeDtypeStruct((rows_part.shape[1], hidden_width), jnp.float32),
         ),
-        in_specs=[anywhere, vmem, vmem, vmem] + [anywhere] * 7,
-        out_specs=(vmem,) * 9,
+        in_specs=[anywhere, vmem, vmem, vmem] + [anywhere] * 5,
+        out_specs=(vmem,) * 7,
         scratch_shapes=[
             pltpu.VMEM((2, rows, width), jnp.bfloat16),
             pltpu.VMEM((2, rows, width), jnp.bfloat16),
@@ -744,7 +823,7 @@
             pltpu.VMEM((8, width), jnp.float32),
             *SUM_SEMS,
             *[ref for _, _, scratch in plan for ref in scratch],
-            *collect_scratch(*parts[0].shape[1:]) * 3,
+            *collect_scratch(*rows_part.shape[1:]),
         ],
         compiler_params=pltpu.CompilerParams(
             collective_id=3, has_side_effects=True, vmem_limit_bytes=48 * 2**20
@@ -758,7 +837,7 @@
         few.reshape(*leading, *few.shape[1:]),
         side_y,
         side_o,
-        *parts,
+        rows_part,
     )
 
 
@@ -1054,20 +1133,41 @@
     grad_gate_low = once(grad_gate)
     grad_up_low = once(grad_up)
 
-    out_part = contract_last(hidden_low, down_cols).astype(jnp.bfloat16)
-    out_part, hidden_low, grad_gate_low, grad_up_low = lax.optimization_barrier(
-        (out_part, hidden_low, grad_gate_low, grad_up_low)
-    )
-    back_part = (
-        contract_last(grad_gate_low, gate_cols) + contract_last(grad_up_low, up_cols)
-    ).astype(jnp.bfloat16)
+    back_part = product_pair(grad_gate_low, grad_up_low, gate_cols, up_cols)
     down_grad = contract_first(cot_all, hidden_low).astype(jnp.bfloat16)
-    back_part, down_grad = lax.optimization_barrier((back_part, down_grad))
-    down_rows = own_rows(down_grad)
+    gate_grad = contract_first(normed2_all, grad_gate_low).astype(jnp.bfloat16)
+    down_rows, gate_rows = own_rows(down_grad), own_rows(gate_grad)
+    back_part, _, _ = lax.optimization_barrier((back_part, down_grad, gate_grad))
     grad_resid, grad_lru_low, grad_gain2 = back_pass(back_part, resid, cot_own, norm2_gain)
     grad_lru_low = grad_lru_low.reshape(tok_rows, -1)
-    gate_rows = own_rows(contract_first(normed2_all, grad_gate_low))
-    up_rows = own_rows(contract_first(normed2_all, grad_up_low))
+    grad_product = contract_last(grad_lru_low, proj_out)
+    grad_states = grad_product * gelu_y
+    grad_y_low = gelu_pull(grad_product * states)[0].astype(jnp.bfloat16)
+    total_grad, _ = scan_stream(decay, grad_states, True)
+    total_grad, late_y, late_lru = lax.optimization_barrier(
+        (total_grad, grad_y_low, grad_lru_low)
+    )
+
+    def token_sum(left_rows, right_rows):
+        return contract_first(left_rows, right_rows).astype(jnp.bfloat16)
+
+    def per_device(rows):
+        return rows.reshape(dp_size, rows.shape[0] // dp_size, rows.shape[1])
+
+    dims = list(range(dp_size.bit_length() - 1))[::-1]
+
+    def by_bits(grad):
+        return grad.reshape(*[2] * len(dims), grad.shape[0] // dp_size, grad.shape[1])
+
+    keep_y, away_y = parted(by_bits(token_sum(normed_low, late_y)), dims, 0)
+    keep_o, away_o = parted(by_bits(token_sum(late_lru, product_low)), dims, 1)
+    total_grad, away_y, away_o, late_up, late_hidden = lax.optimization_barrier(
+        (total_grad, away_y, away_o, grad_up_low, hidden_low)
+    )
+    came_y, came_o = flipped(away_y, "dp", 1), flipped(away_o, "dp", 2)
+    up_grad = contract_first(normed2_all, late_up)
+    out_part = contract_last(late_hidden, down_cols).astype(jnp.bfloat16)
+    up_rows = own_rows(up_grad)
     block_out = resid + lax.psum_scatter(
         out_part,
         everyone,
@@ -1075,34 +1175,16 @@
         scatter_dimension=0,
         tiled=True,
     ).astype(jnp.float32)
-
-    grad_product = contract_last(grad_lru_low, proj_out)
-    grad_states = grad_product * gelu_y
-    grad_y_low = gelu_pull(grad_product * states)[0].astype(jnp.bfloat16)
-    total_grad, _ = scan_stream(decay, grad_states, True)
-    total_grad, late_y, late_lru = lax.optimization_barrier(
-        (total_grad, grad_y_low, grad_lru_low)
-    )
-
-    def token_sum(left_rows, right_rows):
-        return contract_first(left_rows, right_rows).astype(jnp.bfloat16)
-
-    def per_device(rows):
-        return rows.reshape(dp_size, rows.shape[0] // dp_size, rows.shape[1])
-
-    dims = list(range(dp_size.bit_length() - 1))[::-1]
-
-    def by_bits(grad):
-        return grad.reshape(*[2] * len(dims), grad.shape[0] // dp_size, grad.shape[1])
-
-    keep_y, away_y = parted(by_bits(token_sum(normed_low, late_y)), dims, 0)
-    keep_o, away_o = parted(by_bits(token_sum(late_lru, product_low)), dims, 1)
-    total_grad, away_y, away_o = lax.optimization_barrier((total_grad, away_y, away_o))
-    came_y, came_o = flipped(away_y, "dp", 1), flipped(away_o, "dp", 2)
     back_y = contract_last(late_y, proj_y)
     conv_direct, grad_pre_input, grad_pre_recur, grad_param = recur_pull(
         (total_grad * previous, total_grad)
     )
+
+    grad_pre_input, grad_pre_recur, *rows = lax.optimization_barrier(
+        (grad_pre_input, grad_pre_recur, down_rows, gate_rows)
+    )
+    row_pieces = picked(*rows)
+    row_pieces = exchanged(row_pieces)
 
     def gate_back(weight, grad_pre):
         grad_pre_low = grad_pre.astype(jnp.bfloat16)
@@ -1154,7 +1236,7 @@
     few = jnp.concatenate(
         [per_device(wide.astype(jnp.bfloat16)), per_device(sums.astype(jnp.bfloat16))], axis=1
     )
-    grad_tokens, grad_gain1, grad_proj_x, reduced, grad_proj_y, grad_out, *grad_rows = last_pass(
+    grad_tokens, grad_gain1, grad_proj_x, reduced, grad_proj_y, grad_out, grad_mlp_up = last_pass(
         (contract_last(grad_x_low, proj_x) + back_y).astype(jnp.bfloat16),
         tok_own,
         grad_resid,
@@ -1163,12 +1245,13 @@
         few,
         side_y,
         side_o,
-        (down_rows, gate_rows, up_rows),
+        up_rows,
         hidden_width,
     )
-    grad_mlp_down, grad_mlp_gate, grad_mlp_up = grad_rows
     grad_proj_out = grad_out.T
     shared, gains = final_pass(reduced, grad_gain1, grad_gain2)
+    gains, *row_pieces = lax.optimization_barrier((gains, *row_pieces))
+    grad_mlp_down, grad_mlp_gate = joined(row_pieces, hidden_width)
     wide_rows = 2 * block_width // dp_size
     wide = shared[:, :wide_rows].reshape(2 * block_width, chan_width).astype(jnp.float32)
     small = shared[:, wide_rows:].reshape(dp_size * 16, chan_width).astype(jnp.float32)

time: 773 us -> 756 us (0.978)
  matrix products: 156 us -> 124 us
  Pallas kernels: 406 us -> 428 us
  waiting for transfers between devices: 36.7 us -> 20.7 us
  starting transfers between devices: 16.6 us -> 28.2 us
    dot_general x8 -> x6, matrix products: 49.1 us -> 23.9 us  [contract_last(): lax.dot_general(left_rows, right_rows, (((1,), (1,)), ((), ())), preferre...]
    pallas_call x0 -> x3, Pallas kernels: none -> 18.3 us  [the longest x1 12.5 us: product_pair(): pl.pallas_call(product_pair_kernel, name='product_pair', grid=(rows // bl...]
    ppermute x10 -> x13, waiting for transfers between devices: 34.4 us -> 19.1 us  [flipped(): lax.ppermute(array, axis, [(i, i ^ mask) for i in range(lax.axis_size(axi...]
    reduce_scatter x3, starting transfers between devices: 0.53 us -> 9.32 us  [own_rows(): lax.psum_scatter(grad, 'dp', axis_index_groups=high_groups, scatter_dimen...]
    reduce_sum x1, other arithmetic: 7.97 us -> 0.15 us  [inner(): jnp.sum(grad_pre_input, axis=0)[None]]
    unnamed x227 -> x239, local copies, waits for them, and re-layouts: 45.5 us -> 46.8 us
  transfers between devices with their start and end apart: 19 -> 22, of which waited for: 4 -> 3; matrix products, arithmetic and copies ran while one was open for 27% -> 24% of each run, Pallas kernels for 53% -> 57%
where the time goes in v1:
time: 756 us; the launch traced here: 748 us
  Pallas kernels  428 us (57%)
  matrix products  124 us (16%)
  local copies, waits for them, and re-layouts  78.7 us (10%)
  other arithmetic  52 us (7%)
  starting transfers between devices  28.2 us (4%)
  waiting for transfers between devices  20.7 us (3%)
  between operations  16 us (2%)
    pallas_call x1, Pallas kernels, last_pass(): pl.pallas_call(functools.partial(last_kernel, plan), name='last', out_sha...  159 us
    pallas_call x1, Pallas kernels, middle(): pl.pallas_call(middle_kernel, name='middle', out_shape=(jax.ShapeDtypeStr...  109 us
    pallas_call x1, Pallas kernels, back_pass(): pl.pallas_call(back_kernel, name='back', out_shape=(jax.ShapeDtypeStruct(...  83.2 us
    dot_general x9, matrix products, matmul(): return jnp.dot(left_rows, right_rows, preferred_element_type=jnp.float32)  54.9 us
    unnamed x239, local copies, waits for them, and re-layouts  46.8 us
    dot_general x8, matrix products, contract_first(): lax.dot_general(left_rows, right_rows, (((0,), (0,)), ((), ())), preferre...  40.3 us
    pallas_call x2, Pallas kernels, scan_stream(): pl.pallas_call(functools.partial(scan_kernel, n, reverse), name='scan_bac...  32 us
    dot_general x6, matrix products, contract_last(): lax.dot_general(left_rows, right_rows, (((1,), (1,)), ((), ())), preferre...  23.9 us
  transfers between devices with their start and end apart: 22, of which 3 were waited for; matrix products, arithmetic and copies ran while one was open for 24% of the time, Pallas kernels for 57%

profile of v1, /device:TPU:0, one launch (start us, length us, event | category | flops | bytes accessed | tf_op | source)
XLA Modules:
  0.0 747.7 jit_solution(8613012063716315447)
XLA Ops:
  10.4 3.0 collective-permute-start.1
  13.4 1.6 collective-permute-start.2
  15.0 1.5 slice.87
  16.5 4.4 collective-permute-start
  25.4 2.3 fusion
  28.3 1.8 constant_dynamic-slice_fusion.4
  32.8 4.0 fusion.2
  37.4 1.6 collective-permute-start.6
  40.1 1.5 fusion.54
  45.7 4.9 convolution_convert_fusion.8
  53.7 2.1 copy.91
  55.7 2.5 fusion.85
  59.5 2.5 copy.136
  62.0 2.5 copy.137
  67.6 5.7 convert_multiply_fusion.3
  73.3 7.2 collective-permute-done.7.refs_3_
  80.5 1.7 place.2
  85.0 2.1 constant_dynamic-slice_fusion.3.tok_ref
  87.2 2.0 constant_dynamic-slice_fusion.2.cot_ref
  89.1 14.2 %scan.1 = (f32[512,640]{1,0:T(8,128)S(1)}, f32[1,640]{1,0:T(1,128)S(1)}) custom-call(f32[512,640]{1,0:T(8,128)S(1)} %copy-done.2, f32[512,640]{1,0:T(8,128)S(1)} %copy-done.13), custom_call_target="tpu_custom_call" | custom-call | tf_op jit(solution)/shard_map/scan/pallas_call | solution.py:925
  103.3 5.7 multiply_convert_fusion
  109.1 3.7 convolution_convert_fusion.7
  115.0 1.7 copy-done.14
  116.7 108.7 %middle.1 = (f32[128,2560]{1,0:T(8,128)S(1)}, bf16[2,2,2,2,128,2560]{5,4,3,2,1,0:T(8,128)(2,1)S(1)}, bf16[2,2,2,2,128,2560]{5,4,3,2,1,0:T(8,128)(2,1)}) custom-call(bf16[2,2,128,2560]{3,2,1,0:T(8,128)(2,1)S(1)} %bitcast.105, bf16[128,2560]{1,0:T(8,128)(2,1)S(1)} %copy-done.5, bf16[128,2560]{1,0:T(8,128)(2,1)S(1)} %copy-done.7, f32[1,2560]{1,0:T(1,128)S(1)} %reshape.203.gain_ref), custom_call_target="tpu_custom_call" | custom-call | tf_op jit(solution)/shard_map/middle/pallas_call | solution.py:457
  226.5 3.9 copy-done.40
  230.4 10.4 %fusion.88 = f32[2048,512]{1,0:T(8,128)} fusion(bf16[2048,2560]{1,0:T(8,128)(2,1)} %bitcast.110, bf16[2560,512]{1,0:T(8,128)(2,1)} %bitcast.116), kind=kOutput, calls=%fused_computation.177 | convolution fusion | flops 5368709120 | bytes 17301504 | tf_op jit(solution)/shard_map/dot_general | solution.py:45
  240.8 10.4 %fusion.87 = f32[2048,512]{1,0:T(8,128)} fusion(bf16[2048,2560]{1,0:T(8,128)(2,1)} %bitcast.153, bf16[2560,512]{1,0:T(8,128)(2,1)} %bitcast.155), kind=kOutput, calls=%fused_computation.176 | convolution fusion | flops 5368709120 | bytes 17301504 | tf_op jit(solution)/shard_map/dot_general | solution.py:45
  251.3 1.5 all-gather.6.cloned.1.call-done
  252.8 15.4 %select_convert_fusion = (bf16[2048,512]{1,0:T(8,128)(2,1)}, bf16[2048,512]{1,0:T(8,128)(2,1)S(1)}, bf16[2048,512]{1,0:T(8,128)(2,1)}) fusion(pred[512]{0:T(512)(128)(4,1)S(1)} %iota_compare_fusion, f32[2048,512]{1,0:T(8,128)} %fusion.88, f32[2048,512]{1,0:T(8,128)} %fusion.87, bf16[2048,2560]{1,0:T(8,128)(2,1)} %bitcast.111, bf16[2560,512]{1,0:T(8,128)(2,1)} %bitcast.118), kind=kOutput, calls=%fused_computation.24 | convolution fusion | flops 5399117824 | bytes 27787776 | tf_op jit(solution)/shard_map/dot_general | solution.py:45
  268.2 11.7 %convolution_convert_fusion.5 = bf16[2560,512]{1,0:T(8,128)(2,1)} fusion(bf16[2048,2560]{1,0:T(8,128)(2,1)} %bitcast.112, bf16[2048,512]{1,0:T(8,128)(2,1)S(1)} %get-tuple-element.168.left1_ref), kind=kOutput, calls=%fused_computation.13 | convolution fusion | flops 5370019840 | bytes 15204352 | tf_op jit(solution)/shard_map/dot_general | solution.py:39
  280.0 10.1 %convolution_convert_fusion.6 = bf16[2560,512]{1,0:T(8,128)(2,1)} fusion(bf16[2048,2560]{1,0:T(8,128)(2,1)} %bitcast.154, bf16[2048,512]{1,0:T(8,128)(2,1)} %get-tuple-element.114), kind=kOutput, calls=%fused_computation.14 | convolution fusion | flops 5370019840 | bytes 15204352 | tf_op jit(solution)/shard_map/dot_general | solution.py:39
  290.1 9.2 %reduce-scatter.11.cloned.1.call-start = ((), (), s32[]{:S(2)}) async-start(), calls=%async_computation.10 | async-start | bytes 3932160 | tf_op jit(solution)/shard_map/reduce_scatter | solution.py:1035
  299.4 1.7 copy-done.41
  301.1 1.7 copy-done.42
  302.9 1.6 copy-done.43
  304.4 1.6 copy-done.45
  306.0 12.5 %product_pair.1 = bf16[2048,2560]{1,0:T(8,128)(2,1)S(1)} custom-call(bf16[2048,512]{1,0:T(8,128)(2,1)S(1)} %copy-done.45, bf16[2048,512]{1,0:T(8,128)(2,1)S(1)} %copy-done.43, bf16[2560,512]{1,0:T(8,128)(2,1)S(1)} %bitcast.117, bf16[2560,512]{1,0:T(8,128)(2,1)S(1)} %bitcast.119), custom_call_target="tpu_custom_call" | custom-call | flops 10737418240 | bytes 19922944 | tf_op jit(solution)/shard_map/product_pair/pallas_call | solution.py:497
  318.5 3.9 copy-done.4
  322.4 83.2 %back.1 = (f32[128,2560]{1,0:T(8,128)S(1)}, bf16[2,2,128,2560]{3,2,1,0:T(8,128)(2,1)S(1)}, f32[1,2560]{1,0:T(1,128)S(1)}) custom-call(bf16[2,2,2,2,128,2560]{5,4,3,2,1,0:T(8,128)(2,1)} %bitcast.104, f32[128,2560]{1,0:T(8,128)S(1)} %copy-done.10, bf16[128,2560]{1,0:T(8,128)(2,1)S(1)} %copy-done.8, f32[1,2560]{1,0:T(1,128)S(1)} %reshape.203.gain_ref), custom_call_target="tpu_custom_call" | custom-call | tf_op jit(solution)/shard_map/back/pallas_call | solution.py:631
  405.7 2.9 fusion.19
  408.6 17.8 %scan_back.1 = (f32[512,640]{1,0:T(8,128)S(1)}, f32[1,640]{1,0:T(1,128)}) custom-call(f32[512,640]{1,0:T(8,128)S(1)} %copy-done.3, f32[512,640]{1,0:T(8,128)S(1)} %get-tuple-element.171.refs_1_), custom_call_target="tpu_custom_call" | custom-call | tf_op jit(solution)/shard_map/scan_back/pallas_call | solution.py:925
  426.4 2.2 convolution_convert_fusion.2
  432.3 2.3 convolution_convert_fusion.3
  434.6 1.7 copy-done.69
  437.6 7.1 convolution_convert_fusion.4
  444.8 10.5 %convolution_convert_fusion = bf16[2048,2560]{1,0:T(8,128)(2,1)} fusion(bf16[2048,512]{1,0:T(8,128)(2,1)} %get-tuple-element.114, bf16[2560,512]{1,0:T(8,128)(2,1)} %bitcast.156), kind=kOutput, calls=%fused_computation | convolution fusion | flops 5373952000 | bytes 15204352 | tf_op jit(solution)/shard_map/dot_general | solution.py:33
  457.2 7.5 %multiply_reduce_fusion = (f32[640]{0:T(1024)S(1)}, f32[512,640]{1,0:T(8,128)S(1)}) fusion(f32[640]{0:T(1024)S(1)} %copy-done.88, f32[512,512]{1,0:T(8,128)} %copy.136, f32[512,128]{1,0:T(8,128)S(1)} %copy-done.57, pred[]{:T(512)S(6)} %eq.27, f32[512,640]{1,0:T(8,128)S(1)} %get-tuple-element.115, f32[511,640]{1,0:T(8,128)S(1)} %bitcast.106, ...), kind=kLoop, calls=%fused_computation.71 | loop fusion | flops 15072640 | bytes 11826177 | tf_op jit(solution)/shard_map/transpose(jvp())/reduce_sum | solution.py:1102
  464.8 1.6 fusion.21
  467.3 4.5 fusion.90
  471.8 3.5 fusion.20
  480.8 1.6 collective-permute-start.13
  492.9 1.5 fusion.48
  500.2 2.1 pad_maximum_fusion.1
  503.9 5.7 multiply_reduce_fusion.4
  511.5 11.9 %collective-permute-done.10 = bf16[2,2,320,640]{3,2,1,0:T(8,128)(2,1)} collective-permute-done((bf16[2,2,320,640]{3,2,1,0:T(8,128)(2,1)}, bf16[2,2,320,640]{3,2,1,0:T(8,128)(2,1)}, u32[]{:S(2)}, u32[]{:S(2)}) %collective-permute-start.10) | collective-permute-done | bytes 1638432 | tf_op jit(solution)/shard_map/ppermute | solution.py:55
  525.1 2.3 pad_add_fusion
  527.9 3.2 fusion.11.o_ref
  531.0 3.1 fusion.12.y_ref
  534.3 4.0 convolution_convert_fusion.1
  538.3 3.8 add_convert_fusion
  542.1 158.6 %last.1 = (f32[128,2560]{1,0:T(8,128)S(1)}, f32[1,2560]{1,0:T(1,128)S(1)}, f32[320,640]{1,0:T(8,128)S(1)}, bf16[80,640]{1,0:T(8,128)(2,1)S(1)}, f32[320,640]{1,0...) custom-call(bf16[2,2,128,2560]{3,2,1,0:T(8,128)(2,1)} %bitcast.142, bf16[128,2560]{1,0:T(8,128)(2,1)S(1)} %copy-done.6, ...), custom_call_target="tpu_custom_call" | custom-call | tf_op jit(solution)/shard_map/last/pallas_call | solution.py:805
  701.6 21.8 %final.1 = (bf16[8,80,640]{2,1,0:T(8,128)(2,1)S(1)}, f32[2,2560]{1,0:T(2,128)S(1)}) custom-call(bf16[80,640]{1,0:T(8,128)(2,1)S(1)} %get-tuple-element.127.small_ref, f32[1,2560]{1,0:T(1,128)S(1)} %get-tuple-element.128.gain1_ref, f32[1,2560]{1,0:T(1,128)S(1)} %get-tuple-element.129.gain2_ref), custom_call_target="tpu_custom_call" | custom-call | tf_op jit(solution)/shard_map/final/pallas_call | solution.py:341
  726.1 4.4 join.1
  731.2 2.4 convert_add_fusion.2
  (342 shorter events, 76.3 us)
Async XLA Ops:
  7.2 101.9 %copy-start = (bf16[640,2560]{1,0:T(8,128)(2,1)S(1)}, bf16[640,2560]{1,0:T(8,128)(2,1)}, u32[]{:S(2)}) copy-start(bf16[640,2560]{1,0:T(8,128)(2,1)} %param.30) | copy-start | bytes 9830404
  7.2 223.2 %all-gather.8.cloned.1.call-start = ((), (), s32[]{:S(2)}) async-start(), calls=%async_computation.6 | async-start | bytes 3932160 | tf_op jit(solution)/shard_map/all_gather | solution.py:1028
  8.7 12.2 %copy-start.26 = (bf16[320,1920]{1,0:T(8,128)(2,1)S(1)}, bf16[320,1920]{1,0:T(8,128)(2,1)}, u32[]{:S(2)}) copy-start(bf16[320,1920]{1,0:T(8,128)(2,1)} %refs_0_.3) | copy-start | bytes 3686404
  10.4 31.8 %collective-permute-start.1 = (bf16[1,320,512]{2,1,0:T(8,128)(2,1)}, bf16[1,320,512]{2,1,0:T(8,128)(2,1)}, u32[]{:S(2)}, u32[]{:S(2)}) collective-permute-start(bf16[1,320,512]{2,1,0:T(8,128)(2,1)} %get-tuple-element.84), channel_id=1, source_target_pairs={{0,4},{4,0},{8,12},{12,8},{16,20},{20,16},{24,28},{28,24},{1,5},{5... | collective-permute-start | bytes 983048 | tf_op jit(solution)/shard_map/ppermute | solution.py:55
  13.4 29.8 %collective-permute-start.2 = (bf16[1,320,512]{2,1,0:T(8,128)(2,1)}, bf16[1,320,512]{2,1,0:T(8,128)(2,1)}, u32[]{:S(2)}, u32[]{:S(2)}) collective-permute-start(bf16[1,320,512]{2,1,0:T(8,128)(2,1)} %get-tuple-element.85), channel_id=1, source_target_pairs={{0,8},{4,12},{8,0},{12,4},{16,24},{20,28},{24,16},{28,20},{1,9},{5... | collective-permute-start | bytes 983048 | tf_op jit(solution)/shard_map/ppermute | solution.py:55
  15.0 28.3 %collective-permute-start.3 = (bf16[1,320,512]{2,1,0:T(8,128)(2,1)}, bf16[1,320,512]{2,1,0:T(8,128)(2,1)}, u32[]{:S(2)}, u32[]{:S(2)}) collective-permute-start(bf16[1,320,512]{2,1,0:T(8,128)(2,1)} %get-tuple-element.86), channel_id=1, source_target_pairs={{0,12},{4,8},{8,4},{12,0},{16,28},{20,24},{24,20},{28,16},{1,13},{... | collective-permute-start | bytes 983048 | tf_op jit(solution)/shard_map/ppermute | solution.py:55
  16.5 20.9 %collective-permute-start = (bf16[16,2560]{1,0:T(8,128)(2,1)}, bf16[16,2560]{1,0:T(8,128)(2,1)}, u32[]{:S(2)}, u32[]{:S(2)}) collective-permute-start(bf16[16,2560]{1,0:T(8,128)(2,1)} %slice.87), channel_id=1, source_target_pairs={{0,4},{4,8},{8,12},{12,16},{16,20},{20,24},{24,28},{1,5},{5,9},{9,... | collective-permute-start | bytes 245768 | tf_op jit(solution)/shard_map/ppermute | solution.py:51
  24.5 48.8 %collective-permute-start.5 = (bf16[2,320,512]{2,1,0:T(8,128)(2,1)}, bf16[2,320,512]{2,1,0:T(8,128)(2,1)}, u32[]{:S(2)}, u32[]{:S(2)}) collective-permute-start(bf16[2,320,512]{2,1,0:T(8,128)(2,1)} %get-tuple-element.89), channel_id=1, source_target_pairs={{0,4},{4,0},{8,12},{12,8},{16,20},{20,16},{24,28},{28,24},{1,5},{5... | collective-permute-start | bytes 1966088 | tf_op jit(solution)/shard_map/ppermute | solution.py:55
  27.7 4.3 copy-start.99
  27.7 5.0 copy-start.84
  32.0 26.1 %copy-start.79 = (bf16[256,512]{0,1:T(8,128)(2,1)}, bf16[256,512]{0,1:T(8,128)(2,1)S(1)}, u32[]{:S(2)}) copy-start(bf16[256,512]{0,1:T(8,128)(2,1)S(1)} %copy.96) | copy-start | bytes 786436
  32.7 4.0 copy-start.105
  32.7 4.6 copy-start.103
  32.7 7.4 copy-start.65
  32.7 7.4 copy-start.85
  37.4 35.9 %collective-permute-start.6 = (bf16[2,320,512]{2,1,0:T(8,128)(2,1)}, bf16[2,320,512]{2,1,0:T(8,128)(2,1)}, u32[]{:S(2)}, u32[]{:S(2)}) collective-permute-start(bf16[2,320,512]{2,1,0:T(8,128)(2,1)} %get-tuple-element.90), channel_id=1, source_target_pairs={{0,8},{4,12},{8,0},{12,4},{16,24},{20,28},{24,16},{28,20},{1,9},{5... | collective-permute-start | bytes 1966088 | tf_op jit(solution)/shard_map/ppermute | solution.py:55
  42.2 38.2 %collective-permute-start.7 = (bf16[2,320,512]{2,1,0:T(8,128)(2,1)}, bf16[2,320,512]{2,1,0:T(8,128)(2,1)}, u32[]{:S(2)}, u32[]{:S(2)}) collective-permute-start(bf16[2,320,512]{2,1,0:T(8,128)(2,1)} %get-tuple-element.91), channel_id=1, source_target_pairs={{0,12},{4,8},{8,4},{12,0},{16,28},{20,24},{24,20},{28,16},{1,13},{... | collective-permute-start | bytes 1966088 | tf_op jit(solution)/shard_map/ppermute | solution.py:55
  45.6 195.2 %all-gather.4.cloned.1.call-start = ((), (), s32[]{:S(2)}) async-start(), calls=%async_computation.4 | async-start | bytes 3932160 | tf_op jit(solution)/shard_map/all_gather | solution.py:1028
  45.7 4.9 copy-start.98
  52.8 11.8 %collective-permute-start.4 = (bf16[512,128]{1,0:T(8,128)(2,1)}, bf16[512,128]{1,0:T(8,128)(2,1)}, u32[]{:S(2)}, u32[]{:S(2)}) collective-permute-start(bf16[512,128]{1,0:T(8,128)(2,1)} %constant_dynamic-slice_fusion.5), channel_id=1, source_target_pairs={{0,1},{1,0},{2,3},{3,2},{4,5},{5,4},{6,7},{7,6},{8,9},{9,8},{10,11... | collective-permute-start | bytes 393224 | tf_op jit(solution)/shard_map/ppermute | solution.py:55
  66.0 7.2 copy-start.56
  67.5 5.8 copy-start.61
  67.6 12.9 %copy-start.37 = (bf16[2,320,512]{2,1,0:T(8,128)(2,1)S(1)}, bf16[2,320,512]{2,1,0:T(8,128)(2,1)}, u32[]{:S(2)}) copy-start(bf16[2,320,512]{2,1,0:T(8,128)(2,1)} %copy-done.36) | copy-start | bytes 1966084
  84.3 168.5 %all-gather.6.cloned.1.call-start = ((), (), s32[]{:S(2)}) async-start(), calls=%async_computation.5 | async-start | bytes 3932160 | tf_op jit(solution)/shard_map/all_gather | solution.py:1028
  85.0 4.1 copy-start.2
  85.0 4.1 copy-start.13
  89.1 14.2 %copy-start.72 = (bf16[512,2560]{1,0:T(8,128)(2,1)S(1)}, bf16[512,2560]{1,0:T(8,128)(2,1)}, u32[]{:S(2)}) copy-start(bf16[512,2560]{1,0:T(8,128)(2,1)} %fusion.2) | copy-start | bytes 7864324
  103.3 5.7 copy-start.16
  112.7 362.6 %reduce-scatter.9.cloned.1.call-start = ((), (), s32[]{:S(2)}) async-start(), calls=%async_computation.9 | async-start | bytes 3932160 | tf_op jit(solution)/shard_map/reduce_scatter | solution.py:1035
  226.5 3.9 copy-start.40
  268.2 11.7 %copy-start.44 = (bf16[2048,512]{1,0:T(8,128)(2,1)}, bf16[2048,512]{1,0:T(8,128)(2,1)S(1)}, u32[]{:S(2)}) copy-start(bf16[2048,512]{1,0:T(8,128)(2,1)S(1)} %get-tuple-element.168.left1_ref) | copy-start | bytes 6291460
  280.0 195.3 %reduce-scatter.7.cloned.1.call-start = ((), (), s32[]{:S(2)}) async-start(), calls=%async_computation.8 | async-start | bytes 3932160 | tf_op jit(solution)/shard_map/reduce_scatter | solution.py:1035
  290.1 252.0 %reduce-scatter.11.cloned.1.call-start = ((), (), s32[]{:S(2)}) async-start(), calls=%async_computation.10 | async-start | bytes 3932160 | tf_op jit(solution)/shard_map/reduce_scatter | solution.py:1035
  306.0 16.4 %copy-start.8 = (bf16[128,2560]{1,0:T(8,128)(2,1)S(1)}, bf16[128,2560]{1,0:T(8,128)(2,1)}, u32[]{:S(2)}) copy-start(bf16[128,2560]{1,0:T(8,128)(2,1)} %constant_dynamic-slice_fusion.2.cot_ref) | copy-start | bytes 1966084
  306.0 16.4 %copy-start.10 = (f32[128,2560]{1,0:T(8,128)S(1)}, f32[128,2560]{1,0:T(8,128)}, u32[]{:S(2)}) copy-start(f32[128,2560]{1,0:T(8,128)} %copy-done.9) | copy-start | bytes 3932164
  318.5 3.9 copy-start.4
  322.4 83.2 %copy-start.17 = (f32[512,640]{1,0:T(8,128)S(1)}, f32[512,640]{1,0:T(8,128)}, u32[]{:S(2)}) copy-start(f32[512,640]{1,0:T(8,128)} %copy-done.16) | copy-start | bytes 3932164
  322.4 83.2 %copy-start.109 = (f32[512,640]{1,0:T(8,128)S(1)}, f32[512,640]{1,0:T(8,128)}, u32[]{:S(2)}) copy-start(f32[512,640]{1,0:T(8,128)} %get-tuple-element.191) | copy-start | bytes 3932164
  408.5 21.4 %copy-start.107 = (bf16[512,640]{1,0:T(8,128)(2,1)}, bf16[512,640]{1,0:T(8,128)(2,1)S(1)}, u32[]{:S(2)}) copy-start(bf16[512,640]{1,0:T(8,128)(2,1)S(1)} %get-tuple-element.112) | copy-start | bytes 1966084
  408.5 17.8 %copy-start.111 = (bf16[512,640]{1,0:T(8,128)(2,1)S(1)}, bf16[512,640]{1,0:T(8,128)(2,1)}, u32[]{:S(2)}) copy-start(bf16[512,640]{1,0:T(8,128)(2,1)} %copy-done.110) | copy-start | bytes 1966084
  426.4 11.2 %slice-start = ((s8[10485760]{0:T(1024)(128)(4,1)}), s8[4194304]{0:T(1024)(128)(4,1)S(1)}, s32[]{:S(2)}) async-start(s8[10485760]{0:T(1024)(128)(4,1)} %bitcast.113), calls=%async_computation.11 | async-start | bytes 8388608
  426.4 11.2 %slice-start.1 = ((s8[10485760]{0:T(1024)(128)(4,1)}), s8[4194304]{0:T(1024)(128)(4,1)S(1)}, s32[]{:S(2)}) async-start(s8[10485760]{0:T(1024)(128)(4,1)} %bitcast.113), calls=%async_computation.12 | async-start | bytes 8388608
  432.3 5.3 slice-start.2
  444.7 286.5 %reduce-scatter.5.cloned.1.call-start = ((), (), s32[]{:S(2)}) async-start(), calls=%async_computation.7 | async-start | bytes 11141120 | tf_op jit(solution)/shard_map/reduce_scatter | solution.py:1171
  456.0 67.4 %collective-permute-start.10 = (bf16[2,2,320,640]{3,2,1,0:T(8,128)(2,1)}, bf16[2,2,320,640]{3,2,1,0:T(8,128)(2,1)}, u32[]{:S(2)}, u32[]{:S(2)}) collective-permute-start(bf16[2,2,320,640]{3,2,1,0:T(8,128)(2,1)} %dynamic-slice_bitcast_fusion), channel_id=1, source_target_pairs={{0,8},{4,12},{8,0},{12,4},{16,24},{20,28},{24,16},{28,20},{1,9},{5... | collective-permute-start | bytes 4915208 | tf_op jit(solution)/shard_map/ppermute | solution.py:55
  456.6 66.8 %collective-permute-start.9 = (bf16[2,2,320,640]{3,2,1,0:T(8,128)(2,1)}, bf16[2,2,320,640]{3,2,1,0:T(8,128)(2,1)}, u32[]{:S(2)}, u32[]{:S(2)}) collective-permute-start(bf16[2,2,320,640]{3,2,1,0:T(8,128)(2,1)} %dynamic-slice_bitcast_fusion.1), channel_id=1, source_target_pairs={{0,4},{4,0},{8,12},{12,8},{16,20},{20,16},{24,28},{28,24},{1,5},{5... | collective-permute-start | bytes 4915208 | tf_op jit(solution)/shard_map/ppermute | solution.py:55
  457.2 7.5 %copy-start.100 = (f32[640]{0:T(1024)S(1)}, f32[640]{0:T(1024)}, u32[]{:S(2)}) copy-start(f32[640]{0:T(1024)} %param.29) | copy-start | bytes 7684
  457.2 7.5 %copy-start.50 = (f32[512,512]{1,0:T(8,128)S(1)}, f32[512,512]{1,0:T(8,128)}, u32[]{:S(2)}) copy-start(f32[512,512]{1,0:T(8,128)} %copy.136) | copy-start | bytes 3145732
  467.3 4.5 copy-start.48
  467.3 4.5 copy-start.51
  477.9 4.4 copy-start.60
  479.3 4.3 copy-start.34
  479.3 246.7 %collective-permute-start.12 = (bf16[2,320,512]{2,1,0:T(8,128)(2,1)}, bf16[2,320,512]{2,1,0:T(8,128)(2,1)}, u32[]{:S(2)}, u32[]{:S(2)}) collective-permute-start(bf16[2,320,512]{2,1,0:T(8,128)(2,1)} %get-tuple-element.134), channel_id=1, source_target_pairs={{0,4},{4,0},{8,12},{12,8},{16,20},{20,16},{24,28},{28,24},{1,5},{5... | collective-permute-start | bytes 1966088 | tf_op jit(solution)/shard_map/ppermute | solution.py:55
  480.8 245.2 %collective-permute-start.13 = (bf16[2,320,512]{2,1,0:T(8,128)(2,1)}, bf16[2,320,512]{2,1,0:T(8,128)(2,1)}, u32[]{:S(2)}, u32[]{:S(2)}) collective-permute-start(bf16[2,320,512]{2,1,0:T(8,128)(2,1)} %get-tuple-element.135), channel_id=1, source_target_pairs={{0,8},{4,12},{8,0},{12,4},{16,24},{20,28},{24,16},{28,20},{1,9},{5... | collective-permute-start | bytes 1966088 | tf_op jit(solution)/shard_map/ppermute | solution.py:55
  486.3 16.0 %collective-permute-start.8 = (bf16[512,128]{1,0:T(8,128)(2,1)}, bf16[512,128]{1,0:T(8,128)(2,1)S(1)}, u32[]{:S(2)}, u32[]{:S(2)}) collective-permute-start(bf16[512,128]{1,0:T(8,128)(2,1)} %select_convert_fusion.2), channel_id=1, source_target_pairs={{0,1},{1,0},{2,3},{3,2},{4,5},{5,4},{6,7},{7,6},{8,9},{9,8},{10,11... | collective-permute-start | bytes 393224 | tf_op jit(solution)/shard_map/ppermute | solution.py:55
  502.3 223.7 %collective-permute-start.14 = (bf16[2,320,512]{2,1,0:T(8,128)(2,1)}, bf16[2,320,512]{2,1,0:T(8,128)(2,1)}, u32[]{:S(2)}, u32[]{:S(2)}) collective-permute-start(bf16[2,320,512]{2,1,0:T(8,128)(2,1)} %get-tuple-element.136), channel_id=1, source_target_pairs={{0,12},{4,8},{8,4},{12,0},{16,28},{20,24},{24,20},{28,16},{1,13},{... | collective-permute-start | bytes 1966088 | tf_op jit(solution)/shard_map/ppermute | solution.py:55
  523.4 10.9 %collective-permute-start.11 = (f32[3,640]{1,0:T(4,128)S(1)}, f32[3,640]{1,0:T(4,128)S(1)}, u32[]{:S(2)}, u32[]{:S(2)}) collective-permute-start(f32[3,640]{1,0:T(4,128)S(1)} %pad_add_fusion.1), channel_id=1, source_target_pairs={{4,0},{8,4},{12,8},{16,12},{20,16},{24,20},{28,24},{5,1},{9,5},{13... | collective-permute-start | bytes 23048 | tf_op jit(solution)/shard_map/ppermute | solution.py:51
  534.2 4.1 slice-start.3
  534.2 4.0 copy-start.66
  534.3 4.0 slice-start.4
  701.6 23.3 %copy-start.23 = (f32[128,2560]{1,0:T(8,128)}, f32[128,2560]{1,0:T(8,128)S(1)}, u32[]{:S(2)}) copy-start(f32[128,2560]{1,0:T(8,128)S(1)} %get-tuple-element.212) | copy-start | bytes 3932164
  701.6 23.3 %copy-start.28 = (f32[320,640]{1,0:T(8,128)}, f32[320,640]{1,0:T(8,128)S(1)}, u32[]{:S(2)}) copy-start(f32[320,640]{1,0:T(8,128)S(1)} %get-tuple-element.141) | copy-start | bytes 2457604
  701.6 23.3 %copy-start.30 = (f32[320,640]{1,0:T(8,128)}, f32[320,640]{1,0:T(8,128)S(1)}, u32[]{:S(2)}) copy-start(f32[320,640]{1,0:T(8,128)S(1)} %get-tuple-element.215) | copy-start | bytes 2457604
  726.1 5.1 copy-start.11
  (75 other events, 157.0 us)
Sparse Core Ops, SparseCore 0:
  45.7 68.6 all-gather.7
  116.5 67.0 all-gather.3
  185.7 67.0 all-gather.5
  280.1 65.7 reduce-scatter.8
  348.0 65.6 reduce-scatter.6
  444.8 64.8 reduce-scatter.10
  512.0 181.5 reduce-scatter.4

commit v2 on v1

--- a/solution.py
+++ b/solution.py
@@ -16,7 +16,7 @@
 LINKS = (("dp", FIRST_BIT + 1), ("dp", FIRST_BIT), ("tensor", 1))
 CORE = ("tensor", 0)
 ORDERS = ((0, 1, 2), (0, 2, 1), (1, 2, 0), (2, 0, 1))
-TILES = (8, 3, 5)
+TILES = (9, 5, 3)
 SUM_ORDERS = tuple(order[::-1] for order in ORDERS)
 COLORS = range(len(ORDERS))
 
@@ -196,7 +196,7 @@
 def place_kernel(count, *refs):
     for spot, piece in zip(spots_of_four(), refs[:GROUP]):
         for i in range(count):
-            refs[GROUP + i][spot] = piece[i]
+            refs[GROUP][i, spot] = piece[i]
 
 
 def placed(pieces):
@@ -204,7 +204,7 @@
     return pl.pallas_call(
         functools.partial(place_kernel, count),
         name="place",
-        out_shape=[jax.ShapeDtypeStruct((GROUP, rows, share), jnp.bfloat16)] * count,
+        out_shape=jax.ShapeDtypeStruct((count, GROUP, rows, share), jnp.bfloat16),
         compiler_params=pltpu.CompilerParams(vmem_limit_bytes=24 * 2**20),
     )(*pieces)
 
@@ -1018,15 +1018,10 @@
     hidden_width = mlp_gate.shape[1]
     share = share_width(hidden_width)
 
-    def all_rows(part):
-        rows = part.shape[1]
-        if low_size > 1:
-            part = lax.all_gather(
-                part[:, None], "dp", axis=1, axis_index_groups=low_groups, tiled=True
-            )
-        if high_size > 1:
-            part = lax.all_gather(part, "dp", axis=0, axis_index_groups=high_groups, tiled=True)
-        return part.reshape(dp_size * rows, share)
+    def all_rows(parts):
+        rows = parts.shape[2]
+        parts = lax.all_gather(parts, "dp", axis=1, axis_index_groups=high_groups, tiled=True)
+        return parts.reshape(parts.shape[0], dp_size * rows, share)
 
     def own_rows(grad):
         rows = grad.shape[0] // dp_size
@@ -1054,7 +1049,7 @@
     halo = 16
     normed_low = normalize(tokens)
     normed_low, *gate_pieces = lax.optimization_barrier((normed_low, *gate_pieces))
-    gate_cols = all_rows(*placed(gate_pieces))
+    (gate_cols,) = all_rows(placed(gate_pieces))
     normed_prev = normalize(shifted(tokens[tok_rows - halo :], "dp", 1))
     branch_y = matmul(normed_low, proj_y)
     branch_x = matmul(normed_low, proj_x).astype(jnp.bfloat16)
@@ -1110,7 +1105,7 @@
         recurrence_in, mixed_low.astype(jnp.float32), pre_input, pre_recur, decay_param
     )
     decay, drive, *pieces = lax.optimization_barrier((decay, drive, *pieces))
-    up_cols, down_cols = (all_rows(part) for part in placed(pieces))
+    up_cols, down_cols = all_rows(placed(pieces))
     states, entering = scan_stream(decay, drive, False)
     previous = jnp.concatenate([entering, states[:-1]], axis=0)
     gelu_y, gelu_pull = jax.vjp(gelu_tanh, branch_y)

time: 756 us -> 754 us (level)
  waiting for transfers between devices: 20.7 us -> 30.5 us
  starting transfers between devices: 28.2 us -> 19.7 us
  matrix products: 124 us -> 116 us
    all_gather x3 -> x2, waiting for transfers between devices: 1.5 us -> 12.7 us  [all_rows(): lax.all_gather(parts, 'dp', axis=1, axis_index_groups=high_groups, tiled=...]
    pallas_call x1, Pallas kernels: 12.5 us -> 21.4 us  [product_pair(): pl.pallas_call(product_pair_kernel, name='product_pair', grid=(rows // bl...]
    reduce_scatter x3, starting transfers between devices: 9.32 us -> 0.38 us  [own_rows(): lax.psum_scatter(grad, 'dp', axis_index_groups=high_groups, scatter_dimen...]
    unnamed x239 -> x245, local copies, waits for them, and re-layouts: 46.8 us -> 43.9 us
  transfers between devices with their start and end apart: 22 -> 21, of which waited for: 3 -> 3; matrix products, arithmetic and copies ran while one was open for 24% -> 22% of each run, Pallas kernels for 57% -> 58%
where the time goes in v2:
time: 754 us; the launch traced here: 745 us
  Pallas kernels  433 us (57%)
  matrix products  116 us (15%)
  local copies, waits for them, and re-layouts  77.4 us (10%)
  other arithmetic  52.8 us (7%)
  waiting for transfers between devices  30.5 us (4%)
  starting transfers between devices  19.7 us (3%)
  between operations  16.1 us (2%)
    pallas_call x1, Pallas kernels, last_pass(): pl.pallas_call(functools.partial(last_kernel, plan), name='last', out_sha...  159 us
    pallas_call x1, Pallas kernels, middle(): pl.pallas_call(middle_kernel, name='middle', out_shape=(jax.ShapeDtypeStr...  103 us
    pallas_call x1, Pallas kernels, back_pass(): pl.pallas_call(back_kernel, name='back', out_shape=(jax.ShapeDtypeStruct(...  84.6 us
    dot_general x9, matrix products, matmul(): return jnp.dot(left_rows, right_rows, preferred_element_type=jnp.float32)  51.1 us
    unnamed x245, local copies, waits for them, and re-layouts  43.9 us
    dot_general x8, matrix products, contract_first(): lax.dot_general(left_rows, right_rows, (((0,), (0,)), ((), ())), preferre...  35.6 us
    pallas_call x2, Pallas kernels, scan_stream(): pl.pallas_call(functools.partial(scan_kernel, n, reverse), name='scan_bac...  31.5 us
    dot_general x6, matrix products, contract_last(): lax.dot_general(left_rows, right_rows, (((1,), (1,)), ((), ())), preferre...  23.9 us
  transfers between devices with their start and end apart: 21, of which 3 were waited for; matrix products, arithmetic and copies ran while one was open for 22% of the time, Pallas kernels for 58%

profile of v2, /device:TPU:0, one launch (start us, length us, event | category | flops | bytes accessed | tf_op | source)
XLA Modules:
  0.0 745.3 jit_solution(17153440537441219929)
XLA Ops:
  10.4 3.0 collective-permute-start.1
  13.4 1.6 collective-permute-start.2
  15.0 1.5 slice.89
  16.5 4.4 collective-permute-start
  25.4 2.3 fusion
  28.3 1.8 constant_dynamic-slice_fusion.4
  32.8 4.0 fusion.2
  37.4 1.6 collective-permute-start.6
  40.1 1.5 fusion.54
  45.7 4.9 convolution_convert_fusion.8
  53.7 2.1 copy.91
  55.8 2.5 fusion.86
  59.5 2.5 copy.137
  62.1 2.5 copy.138
  67.6 5.8 convert_multiply_fusion.3
  73.4 7.0 collective-permute-done.7.refs_3_
  80.5 1.7 place.2
  82.2 1.5 copy-done.5
  87.2 14.2 %scan.1 = (f32[512,640]{1,0:T(8,128)S(1)}, f32[1,640]{1,0:T(1,128)S(1)}) custom-call(f32[512,640]{1,0:T(8,128)S(1)} %copy-done.2, f32[512,640]{1,0:T(8,128)S(1)} %copy-done.13), custom_call_target="tpu_custom_call" | custom-call | tf_op jit(solution)/shard_map/scan/pallas_call | solution.py:925
  101.4 5.7 multiply_convert_fusion
  107.1 2.2 convolution_convert_fusion.7
  109.4 103.2 %middle.1 = (f32[128,2560]{1,0:T(8,128)S(1)}, bf16[2,2,2,2,128,2560]{5,4,3,2,1,0:T(8,128)(2,1)S(1)}, bf16[2,2,2,2,128,2560]{5,4,3,2,1,0:T(8,128)(2,1)}) custom-call(bf16[2,2,128,2560]{3,2,1,0:T(8,128)(2,1)S(1)} %bitcast.109, bf16[128,2560]{1,0:T(8,128)(2,1)S(1)} %constant_dynamic-slice_fusion.3.tok_ref, ...), custom_call_target="tpu_custom_call" | custom-call | tf_op jit(solution)/shard_map/middle/pallas_call | solution.py:457
  213.6 3.9 copy-done.39
  217.6 10.3 %fusion.89 = f32[2048,512]{1,0:T(8,128)} fusion(bf16[2048,2560]{1,0:T(8,128)(2,1)} %bitcast.114, bf16[2560,512]{1,0:T(8,128)(2,1)} %bitcast.122), kind=kOutput, calls=%fused_computation.178 | convolution fusion | flops 5368709120 | bytes 17301504 | tf_op jit(solution)/shard_map/dot_general | solution.py:45
  227.9 12.7 %all-gather.3.cloned.1.call-done = bf16[2,8,320,512]{3,2,1,0:T(8,128)(2,1)} async-done(((bf16[2,4,320,512]{3,2,1,0:T(8,128)(2,1)}), bf16[2,8,320,512]{3,2,1,0:T(8,128)(2,1)}) %all-gather.3.cloned.1.call-update) | async-done | bytes 5242896 | tf_op jit(solution)/shard_map/all_gather | solution.py:1023
  240.6 3.0 fusion.82
  243.7 11.5 %fusion.88 = f32[2048,512]{1,0:T(8,128)} fusion(bf16[2048,2560]{1,0:T(8,128)(2,1)} %bitcast.159, bf16[2560,512]{1,0:T(8,128)(2,1)S(1)} %bitcast.142), kind=kOutput, calls=%fused_computation.177 | convolution fusion | flops 5368709120 | bytes 17301504 | tf_op jit(solution)/shard_map/dot_general | solution.py:45
  255.3 12.0 %select_convert_fusion = (bf16[2048,512]{1,0:T(8,128)(2,1)}, bf16[2048,512]{1,0:T(8,128)(2,1)S(1)}, bf16[2048,512]{1,0:T(8,128)(2,1)}) fusion(pred[512]{0:T(512)(128)(4,1)S(1)} %iota_compare_fusion, f32[2048,512]{1,0:T(8,128)S(1)} %copy-done.111, f32[2048,512]{1,0:T(8,128)} %fusion.88, bf16[2048,2560]{1,0:T(8,128)(2,1)S(1)} %bitcast.117, ...), kind=kOutput, calls=%fused_computation.24 | convolution fusion | flops 5399117824 | bytes 27787776 | tf_op jit(solution)/shard_map/dot_general | solution.py:45
  267.3 7.0 convolution_convert_fusion.5
  274.4 10.1 %convolution_convert_fusion.6 = bf16[2560,512]{1,0:T(8,128)(2,1)} fusion(bf16[2048,2560]{1,0:T(8,128)(2,1)} %bitcast.160, bf16[2048,512]{1,0:T(8,128)(2,1)} %get-tuple-element.110), kind=kOutput, calls=%fused_computation.14 | convolution fusion | flops 5370019840 | bytes 15204352 | tf_op jit(solution)/shard_map/dot_general | solution.py:39
  284.6 1.7 copy-done.15
  286.4 1.7 copy-done.40
  288.1 1.6 copy-done.41
  289.7 1.6 copy-done.43
  291.3 21.4 %product_pair.1 = bf16[2048,2560]{1,0:T(8,128)(2,1)S(1)} custom-call(bf16[2048,512]{1,0:T(8,128)(2,1)S(1)} %copy-done.43, bf16[2048,512]{1,0:T(8,128)(2,1)S(1)} %copy-done.41, bf16[2560,512]{1,0:T(8,128)(2,1)S(1)} %bitcast.123, bf16[2560,512]{1,0:T(8,128)(2,1)S(1)} %bitcast.108), custom_call_target="tpu_custom_call" | custom-call | flops 10737418240 | bytes 19922944 | tf_op jit(solution)/shard_map/product_pair/pallas_call | solution.py:497
  312.7 3.9 copy-done.4
  316.6 84.6 %back.1 = (f32[128,2560]{1,0:T(8,128)S(1)}, bf16[2,2,128,2560]{3,2,1,0:T(8,128)(2,1)S(1)}, f32[1,2560]{1,0:T(1,128)S(1)}) custom-call(bf16[2,2,2,2,128,2560]{5,4,3,2,1,0:T(8,128)(2,1)} %bitcast.105, f32[128,2560]{1,0:T(8,128)S(1)} %copy-done.11, bf16[128,2560]{1,0:T(8,128)(2,1)S(1)} %copy-done.9, f32[1,2560]{1,0:T(1,128)S(1)} %reshape.199.gain_ref), custom_call_target="tpu_custom_call" | custom-call | tf_op jit(solution)/shard_map/back/pallas_call | solution.py:631
  401.3 2.9 fusion.19
  404.3 17.3 %scan_back.1 = (f32[512,640]{1,0:T(8,128)S(1)}, f32[1,640]{1,0:T(1,128)}) custom-call(f32[512,640]{1,0:T(8,128)S(1)} %copy-done.3, f32[512,640]{1,0:T(8,128)S(1)} %get-tuple-element.169.refs_1_), custom_call_target="tpu_custom_call" | custom-call | tf_op jit(solution)/shard_map/scan_back/pallas_call | solution.py:925
  421.6 2.2 convolution_convert_fusion.2
  423.9 1.7 copy-done.65
  427.9 2.3 convolution_convert_fusion.3
  430.2 1.7 copy-done.67
  433.2 7.1 convolution_convert_fusion.4
  440.4 10.5 %convolution_convert_fusion = bf16[2048,2560]{1,0:T(8,128)(2,1)} fusion(bf16[2048,512]{1,0:T(8,128)(2,1)} %get-tuple-element.110, bf16[2560,512]{1,0:T(8,128)(2,1)} %bitcast.143), kind=kOutput, calls=%fused_computation | convolution fusion | flops 5373952000 | bytes 15204352 | tf_op jit(solution)/shard_map/dot_general | solution.py:33
  453.6 7.6 %multiply_reduce_fusion = (f32[640]{0:T(1024)S(1)}, f32[512,640]{1,0:T(8,128)S(1)}) fusion(f32[640]{0:T(1024)S(1)} %copy-done.87, f32[512,512]{1,0:T(8,128)} %copy.137, f32[512,128]{1,0:T(8,128)S(1)} %copy-done.55, pred[]{:T(512)S(6)} %eq.27, f32[512,640]{1,0:T(8,128)S(1)} %get-tuple-element.111, f32[511,640]{1,0:T(8,128)S(1)} %bitcast.110, ...), kind=kLoop, calls=%fused_computation.71 | loop fusion | flops 15072640 | bytes 11826177 | tf_op jit(solution)/shard_map/transpose(jvp())/reduce_sum | solution.py:1097
  461.2 1.6 fusion.21
  463.7 4.5 fusion.91
  468.3 3.5 fusion.20
  476.4 1.6 collective-permute-start.13
  488.6 1.5 fusion.48
  490.1 1.4 fusion.45
  495.8 2.1 pad_maximum_fusion.1
  500.3 5.8 multiply_reduce_fusion.4
  508.0 10.6 %collective-permute-done.10 = bf16[2,2,320,640]{3,2,1,0:T(8,128)(2,1)} collective-permute-done((bf16[2,2,320,640]{3,2,1,0:T(8,128)(2,1)}, bf16[2,2,320,640]{3,2,1,0:T(8,128)(2,1)}, u32[]{:S(2)}, u32[]{:S(2)}) %collective-permute-start.10) | collective-permute-done | bytes 1638432 | tf_op jit(solution)/shard_map/ppermute | solution.py:55
  520.4 2.3 pad_add_fusion
  523.1 3.2 fusion.11.o_ref
  526.3 3.1 fusion.12.y_ref
  529.6 4.0 convolution_convert_fusion.1
  533.5 3.8 add_convert_fusion
  538.4 158.6 %last.1 = (f32[128,2560]{1,0:T(8,128)S(1)}, f32[1,2560]{1,0:T(1,128)S(1)}, f32[320,640]{1,0:T(8,128)S(1)}, bf16[80,640]{1,0:T(8,128)(2,1)S(1)}, f32[320,640]{1,0...) custom-call(bf16[2,2,128,2560]{3,2,1,0:T(8,128)(2,1)} %bitcast.148, bf16[128,2560]{1,0:T(8,128)(2,1)S(1)} %copy-done.7, ...), custom_call_target="tpu_custom_call" | custom-call | tf_op jit(solution)/shard_map/last/pallas_call | solution.py:805
  698.1 22.5 %final.1 = (bf16[8,80,640]{2,1,0:T(8,128)(2,1)S(1)}, f32[2,2560]{1,0:T(2,128)S(1)}) custom-call(bf16[80,640]{1,0:T(8,128)(2,1)S(1)} %get-tuple-element.123.small_ref, f32[1,2560]{1,0:T(1,128)S(1)} %get-tuple-element.124.gain1_ref, f32[1,2560]{1,0:T(1,128)S(1)} %get-tuple-element.125.gain2_ref), custom_call_target="tpu_custom_call" | custom-call | tf_op jit(solution)/shard_map/final/pallas_call | solution.py:341
  723.4 4.3 join.1
  728.4 2.8 convert_add_fusion.2
  (347 shorter events, 73.8 us)
Async XLA Ops:
  7.2 100.0 %copy-start = (bf16[640,2560]{1,0:T(8,128)(2,1)S(1)}, bf16[640,2560]{1,0:T(8,128)(2,1)}, u32[]{:S(2)}) copy-start(bf16[640,2560]{1,0:T(8,128)(2,1)} %param.30) | copy-start | bytes 9830404
  7.2 210.4 %all-gather.5.cloned.1.call-start = ((), (), s32[]{:S(2)}) async-start(), calls=%async_computation.5 | async-start | bytes 3932160 | tf_op jit(solution)/shard_map/all_gather | solution.py:1023
  8.7 12.2 %copy-start.25 = (bf16[320,1920]{1,0:T(8,128)(2,1)S(1)}, bf16[320,1920]{1,0:T(8,128)(2,1)}, u32[]{:S(2)}) copy-start(bf16[320,1920]{1,0:T(8,128)(2,1)} %refs_0_.3) | copy-start | bytes 3686404
  10.4 31.8 %collective-permute-start.1 = (bf16[1,320,512]{2,1,0:T(8,128)(2,1)}, bf16[1,320,512]{2,1,0:T(8,128)(2,1)}, u32[]{:S(2)}, u32[]{:S(2)}) collective-permute-start(bf16[1,320,512]{2,1,0:T(8,128)(2,1)} %get-tuple-element.82), channel_id=1, source_target_pairs={{0,4},{4,0},{8,12},{12,8},{16,20},{20,16},{24,28},{28,24},{1,5},{5... | collective-permute-start | bytes 983048 | tf_op jit(solution)/shard_map/ppermute | solution.py:55
  13.4 29.9 %collective-permute-start.2 = (bf16[1,320,512]{2,1,0:T(8,128)(2,1)}, bf16[1,320,512]{2,1,0:T(8,128)(2,1)}, u32[]{:S(2)}, u32[]{:S(2)}) collective-permute-start(bf16[1,320,512]{2,1,0:T(8,128)(2,1)} %get-tuple-element.83), channel_id=1, source_target_pairs={{0,8},{4,12},{8,0},{12,4},{16,24},{20,28},{24,16},{28,20},{1,9},{5... | collective-permute-start | bytes 983048 | tf_op jit(solution)/shard_map/ppermute | solution.py:55
  15.0 28.3 %collective-permute-start.3 = (bf16[1,320,512]{2,1,0:T(8,128)(2,1)}, bf16[1,320,512]{2,1,0:T(8,128)(2,1)}, u32[]{:S(2)}, u32[]{:S(2)}) collective-permute-start(bf16[1,320,512]{2,1,0:T(8,128)(2,1)} %get-tuple-element.84), channel_id=1, source_target_pairs={{0,12},{4,8},{8,4},{12,0},{16,28},{20,24},{24,20},{28,16},{1,13},{... | collective-permute-start | bytes 983048 | tf_op jit(solution)/shard_map/ppermute | solution.py:55
  16.5 20.9 %collective-permute-start = (bf16[16,2560]{1,0:T(8,128)(2,1)}, bf16[16,2560]{1,0:T(8,128)(2,1)}, u32[]{:S(2)}, u32[]{:S(2)}) collective-permute-start(bf16[16,2560]{1,0:T(8,128)(2,1)} %slice.89), channel_id=1, source_target_pairs={{0,4},{4,8},{8,12},{12,16},{16,20},{20,24},{24,28},{1,5},{5,9},{9,... | collective-permute-start | bytes 245768 | tf_op jit(solution)/shard_map/ppermute | solution.py:51
  24.5 49.0 %collective-permute-start.5 = (bf16[2,320,512]{2,1,0:T(8,128)(2,1)}, bf16[2,320,512]{2,1,0:T(8,128)(2,1)}, u32[]{:S(2)}, u32[]{:S(2)}) collective-permute-start(bf16[2,320,512]{2,1,0:T(8,128)(2,1)} %get-tuple-element.87), channel_id=1, source_target_pairs={{0,4},{4,0},{8,12},{12,8},{16,20},{20,16},{24,28},{28,24},{1,5},{5... | collective-permute-start | bytes 1966088 | tf_op jit(solution)/shard_map/ppermute | solution.py:55
  27.7 4.3 copy-start.98
  27.7 5.0 copy-start.83
  32.0 26.2 %copy-start.78 = (bf16[256,512]{0,1:T(8,128)(2,1)}, bf16[256,512]{0,1:T(8,128)(2,1)S(1)}, u32[]{:S(2)}) copy-start(bf16[256,512]{0,1:T(8,128)(2,1)S(1)} %copy.96) | copy-start | bytes 786436
  32.7 4.7 copy-start.102
  32.7 7.4 copy-start.63
  32.7 7.4 copy-start.84
  37.4 36.0 %collective-permute-start.6 = (bf16[2,320,512]{2,1,0:T(8,128)(2,1)}, bf16[2,320,512]{2,1,0:T(8,128)(2,1)}, u32[]{:S(2)}, u32[]{:S(2)}) collective-permute-start(bf16[2,320,512]{2,1,0:T(8,128)(2,1)} %get-tuple-element.88), channel_id=1, source_target_pairs={{0,8},{4,12},{8,0},{12,4},{16,24},{20,28},{24,16},{28,20},{1,9},{5... | collective-permute-start | bytes 1966088 | tf_op jit(solution)/shard_map/ppermute | solution.py:55
  42.3 38.2 %collective-permute-start.7 = (bf16[2,320,512]{2,1,0:T(8,128)(2,1)}, bf16[2,320,512]{2,1,0:T(8,128)(2,1)}, u32[]{:S(2)}, u32[]{:S(2)}) collective-permute-start(bf16[2,320,512]{2,1,0:T(8,128)(2,1)} %get-tuple-element.89), channel_id=1, source_target_pairs={{0,12},{4,8},{8,4},{12,0},{16,28},{20,24},{24,20},{28,16},{1,13},{... | collective-permute-start | bytes 1966088 | tf_op jit(solution)/shard_map/ppermute | solution.py:55
  45.6 195.0 %all-gather.3.cloned.1.call-start = ((), (), s32[]{:S(2)}) async-start(), calls=%async_computation.4 | async-start | bytes 7864320 | tf_op jit(solution)/shard_map/all_gather | solution.py:1023
  45.7 4.9 copy-start.97
  52.9 11.8 %collective-permute-start.4 = (bf16[512,128]{1,0:T(8,128)(2,1)}, bf16[512,128]{1,0:T(8,128)(2,1)}, u32[]{:S(2)}, u32[]{:S(2)}) collective-permute-start(bf16[512,128]{1,0:T(8,128)(2,1)} %constant_dynamic-slice_fusion.5), channel_id=1, source_target_pairs={{0,1},{1,0},{2,3},{3,2},{4,5},{5,4},{6,7},{7,6},{8,9},{9,8},{10,11... | collective-permute-start | bytes 393224 | tf_op jit(solution)/shard_map/ppermute | solution.py:55
  66.1 7.3 copy-start.54
  67.5 5.9 copy-start.59
  67.6 12.9 %copy-start.36 = (bf16[2,320,512]{2,1,0:T(8,128)(2,1)S(1)}, bf16[2,320,512]{2,1,0:T(8,128)(2,1)}, u32[]{:S(2)}) copy-start(bf16[2,320,512]{2,1,0:T(8,128)(2,1)} %copy-done.35) | copy-start | bytes 1966084
  83.7 388.1 %reduce-scatter.9.cloned.1.call-start = ((), (), s32[]{:S(2)}) async-start(), calls=%async_computation.8 | async-start | bytes 3932160 | tf_op jit(solution)/shard_map/reduce_scatter | solution.py:1030
  85.7 23.6 %copy-start.6 = (bf16[128,2560]{1,0:T(8,128)(2,1)}, bf16[128,2560]{1,0:T(8,128)(2,1)S(1)}, u32[]{:S(2)}) copy-start(bf16[128,2560]{1,0:T(8,128)(2,1)S(1)} %constant_dynamic-slice_fusion.3.tok_ref) | copy-start | bytes 1966084
  87.1 22.2 %copy-start.8 = (bf16[128,2560]{1,0:T(8,128)(2,1)}, bf16[128,2560]{1,0:T(8,128)(2,1)S(1)}, u32[]{:S(2)}) copy-start(bf16[128,2560]{1,0:T(8,128)(2,1)S(1)} %constant_dynamic-slice_fusion.2.cot_ref) | copy-start | bytes 1966084
  87.1 14.3 %copy-start.71 = (bf16[512,2560]{1,0:T(8,128)(2,1)S(1)}, bf16[512,2560]{1,0:T(8,128)(2,1)}, u32[]{:S(2)}) copy-start(bf16[512,2560]{1,0:T(8,128)(2,1)} %fusion.2) | copy-start | bytes 7864324
  101.4 5.7 copy-start.17
  240.6 14.6 %slice-start = ((s8[10485760]{0:T(1024)(128)(4,1)}), s8[4194304]{0:T(1024)(128)(4,1)S(1)}, s32[]{:S(2)}) async-start(s8[10485760]{0:T(1024)(128)(4,1)} %bitcast.115), calls=%async_computation.10 | async-start | bytes 8388608
  243.7 11.6 %copy-start.69 = (bf16[1,8,320,512]{3,2,1,0:T(8,128)(2,1)}, bf16[1,8,320,512]{3,2,1,0:T(8,128)(2,1)S(1)}, u32[]{:S(2)}) copy-start(bf16[1,8,320,512]{3,2,1,0:T(8,128)(2,1)S(1)} %get-tuple-element.167) | copy-start | bytes 7864324
  243.7 11.6 %copy-start.14 = (bf16[1,8,320,512]{3,2,1,0:T(8,128)(2,1)}, bf16[1,8,320,512]{3,2,1,0:T(8,128)(2,1)S(1)}, u32[]{:S(2)}) copy-start(bf16[1,8,320,512]{3,2,1,0:T(8,128)(2,1)S(1)} %get-tuple-element.166) | copy-start | bytes 7864324
  243.7 11.6 %slice-start.1 = ((s8[10485760]{0:T(1024)(128)(4,1)}), s8[4194304]{0:T(1024)(128)(4,1)S(1)}, s32[]{:S(2)}) async-start(s8[10485760]{0:T(1024)(128)(4,1)} %bitcast.115), calls=%async_computation.11 | async-start | bytes 8388608
  243.7 11.6 %slice-start.2 = ((s8[10485760]{0:T(1024)(128)(4,1)}), s8[2097152]{0:T(1024)(128)(4,1)S(1)}, s32[]{:S(2)}) async-start(s8[10485760]{0:T(1024)(128)(4,1)} %bitcast.115), calls=%async_computation.12 | async-start | bytes 4194304
  243.7 11.6 %copy-start.111 = (f32[2048,512]{1,0:T(8,128)S(1)}, f32[2048,512]{1,0:T(8,128)}, u32[]{:S(2)}) copy-start(f32[2048,512]{1,0:T(8,128)} %fusion.89) | copy-start | bytes 12582916
  267.3 7.0 copy-start.42
  274.4 197.4 %reduce-scatter.7.cloned.1.call-start = ((), (), s32[]{:S(2)}) async-start(), calls=%async_computation.7 | async-start | bytes 3932160 | tf_op jit(solution)/shard_map/reduce_scatter | solution.py:1030
  284.5 252.8 %reduce-scatter.11.cloned.1.call-start = ((), (), s32[]{:S(2)}) async-start(), calls=%async_computation.9 | async-start | bytes 3932160 | tf_op jit(solution)/shard_map/reduce_scatter | solution.py:1030
  291.3 25.4 %copy-start.9 = (bf16[128,2560]{1,0:T(8,128)(2,1)S(1)}, bf16[128,2560]{1,0:T(8,128)(2,1)}, u32[]{:S(2)}) copy-start(bf16[128,2560]{1,0:T(8,128)(2,1)} %copy-done.8) | copy-start | bytes 1966084
  291.3 25.4 %copy-start.11 = (f32[128,2560]{1,0:T(8,128)S(1)}, f32[128,2560]{1,0:T(8,128)}, u32[]{:S(2)}) copy-start(f32[128,2560]{1,0:T(8,128)} %copy-done.10) | copy-start | bytes 3932164
  316.6 84.7 %copy-start.18 = (f32[512,640]{1,0:T(8,128)S(1)}, f32[512,640]{1,0:T(8,128)}, u32[]{:S(2)}) copy-start(f32[512,640]{1,0:T(8,128)} %copy-done.17) | copy-start | bytes 3932164
  316.6 84.7 %copy-start.108 = (f32[512,640]{1,0:T(8,128)S(1)}, f32[512,640]{1,0:T(8,128)}, u32[]{:S(2)}) copy-start(f32[512,640]{1,0:T(8,128)} %get-tuple-element.189) | copy-start | bytes 3932164
  404.2 22.7 %copy-start.106 = (bf16[512,640]{1,0:T(8,128)(2,1)}, bf16[512,640]{1,0:T(8,128)(2,1)S(1)}, u32[]{:S(2)}) copy-start(bf16[512,640]{1,0:T(8,128)(2,1)S(1)} %get-tuple-element.108) | copy-start | bytes 1966084
  404.3 17.3 %copy-start.110 = (bf16[512,640]{1,0:T(8,128)(2,1)S(1)}, bf16[512,640]{1,0:T(8,128)(2,1)}, u32[]{:S(2)}) copy-start(bf16[512,640]{1,0:T(8,128)(2,1)} %copy-done.109) | copy-start | bytes 1966084
  421.6 11.6 %slice-start.3 = ((s8[10485760]{0:T(1024)(128)(4,1)}), s8[4194304]{0:T(1024)(128)(4,1)S(1)}, s32[]{:S(2)}) async-start(s8[10485760]{0:T(1024)(128)(4,1)} %bitcast.119), calls=%async_computation.13 | async-start | bytes 8388608
  421.6 11.6 %slice-start.4 = ((s8[10485760]{0:T(1024)(128)(4,1)}), s8[4194304]{0:T(1024)(128)(4,1)S(1)}, s32[]{:S(2)}) async-start(s8[10485760]{0:T(1024)(128)(4,1)} %bitcast.119), calls=%async_computation.14 | async-start | bytes 8388608
  427.9 5.3 slice-start.5
  440.3 288.1 %reduce-scatter.5.cloned.1.call-start = ((), (), s32[]{:S(2)}) async-start(), calls=%async_computation.6 | async-start | bytes 11141120 | tf_op jit(solution)/shard_map/reduce_scatter | solution.py:1166
  451.6 67.0 %collective-permute-start.10 = (bf16[2,2,320,640]{3,2,1,0:T(8,128)(2,1)}, bf16[2,2,320,640]{3,2,1,0:T(8,128)(2,1)}, u32[]{:S(2)}, u32[]{:S(2)}) collective-permute-start(bf16[2,2,320,640]{3,2,1,0:T(8,128)(2,1)} %dynamic-slice_bitcast_fusion), channel_id=1, source_target_pairs={{0,8},{4,12},{8,0},{12,4},{16,24},{20,28},{24,16},{28,20},{1,9},{5... | collective-permute-start | bytes 4915208 | tf_op jit(solution)/shard_map/ppermute | solution.py:55
  452.1 66.5 %collective-permute-start.9 = (bf16[2,2,320,640]{3,2,1,0:T(8,128)(2,1)}, bf16[2,2,320,640]{3,2,1,0:T(8,128)(2,1)}, u32[]{:S(2)}, u32[]{:S(2)}) collective-permute-start(bf16[2,2,320,640]{3,2,1,0:T(8,128)(2,1)} %dynamic-slice_bitcast_fusion.1), channel_id=1, source_target_pairs={{0,4},{4,0},{8,12},{12,8},{16,20},{20,16},{24,28},{28,24},{1,5},{5... | collective-permute-start | bytes 4915208 | tf_op jit(solution)/shard_map/ppermute | solution.py:55
  453.5 7.6 %copy-start.99 = (f32[640]{0:T(1024)S(1)}, f32[640]{0:T(1024)}, u32[]{:S(2)}) copy-start(f32[640]{0:T(1024)} %param.29) | copy-start | bytes 7684
  453.5 7.6 %copy-start.48 = (f32[512,512]{1,0:T(8,128)S(1)}, f32[512,512]{1,0:T(8,128)}, u32[]{:S(2)}) copy-start(f32[512,512]{1,0:T(8,128)} %copy.137) | copy-start | bytes 3145732
  463.7 4.5 copy-start.46
  463.7 4.5 copy-start.49
  475.8 247.5 %collective-permute-start.12 = (bf16[2,320,512]{2,1,0:T(8,128)(2,1)}, bf16[2,320,512]{2,1,0:T(8,128)(2,1)}, u32[]{:S(2)}, u32[]{:S(2)}) collective-permute-start(bf16[2,320,512]{2,1,0:T(8,128)(2,1)} %get-tuple-element.130), channel_id=1, source_target_pairs={{0,4},{4,0},{8,12},{12,8},{16,20},{20,16},{24,28},{28,24},{1,5},{5... | collective-permute-start | bytes 1966088 | tf_op jit(solution)/shard_map/ppermute | solution.py:55
  476.4 246.9 %collective-permute-start.13 = (bf16[2,320,512]{2,1,0:T(8,128)(2,1)}, bf16[2,320,512]{2,1,0:T(8,128)(2,1)}, u32[]{:S(2)}, u32[]{:S(2)}) collective-permute-start(bf16[2,320,512]{2,1,0:T(8,128)(2,1)} %get-tuple-element.131), channel_id=1, source_target_pairs={{0,8},{4,12},{8,0},{12,4},{16,24},{20,28},{24,16},{28,20},{1,9},{5... | collective-permute-start | bytes 1966088 | tf_op jit(solution)/shard_map/ppermute | solution.py:55
  481.9 16.0 %collective-permute-start.8 = (bf16[512,128]{1,0:T(8,128)(2,1)}, bf16[512,128]{1,0:T(8,128)(2,1)S(1)}, u32[]{:S(2)}, u32[]{:S(2)}) collective-permute-start(bf16[512,128]{1,0:T(8,128)(2,1)} %select_convert_fusion.2), channel_id=1, source_target_pairs={{0,1},{1,0},{2,3},{3,2},{4,5},{5,4},{6,7},{7,6},{8,9},{9,8},{10,11... | collective-permute-start | bytes 393224 | tf_op jit(solution)/shard_map/ppermute | solution.py:55
  495.8 4.5 copy-start.47
  495.8 4.5 copy-start.56
  495.8 4.5 copy-start.61
  497.9 225.4 %collective-permute-start.14 = (bf16[2,320,512]{2,1,0:T(8,128)(2,1)}, bf16[2,320,512]{2,1,0:T(8,128)(2,1)}, u32[]{:S(2)}, u32[]{:S(2)}) collective-permute-start(bf16[2,320,512]{2,1,0:T(8,128)(2,1)} %get-tuple-element.132), channel_id=1, source_target_pairs={{0,12},{4,8},{8,4},{12,0},{16,28},{20,24},{24,20},{28,16},{1,13},{... | collective-permute-start | bytes 1966088 | tf_op jit(solution)/shard_map/ppermute | solution.py:55
  518.7 10.9 %collective-permute-start.11 = (f32[3,640]{1,0:T(4,128)S(1)}, f32[3,640]{1,0:T(4,128)S(1)}, u32[]{:S(2)}, u32[]{:S(2)}) collective-permute-start(f32[3,640]{1,0:T(4,128)S(1)} %pad_add_fusion.1), channel_id=1, source_target_pairs={{4,0},{8,4},{12,8},{16,12},{20,16},{24,20},{28,24},{5,1},{9,5},{13... | collective-permute-start | bytes 23048 | tf_op jit(solution)/shard_map/ppermute | solution.py:51
  529.4 4.1 slice-start.6
  698.1 24.0 %copy-start.27 = (f32[320,640]{1,0:T(8,128)}, f32[320,640]{1,0:T(8,128)S(1)}, u32[]{:S(2)}) copy-start(f32[320,640]{1,0:T(8,128)S(1)} %get-tuple-element.137) | copy-start | bytes 2457604
  698.1 24.0 %copy-start.29 = (f32[320,640]{1,0:T(8,128)}, f32[320,640]{1,0:T(8,128)S(1)}, u32[]{:S(2)}) copy-start(f32[320,640]{1,0:T(8,128)S(1)} %get-tuple-element.213) | copy-start | bytes 2457604
  698.1 24.0 %copy-start.31 = (f32[320,640]{1,0:T(8,128)}, f32[320,640]{1,0:T(8,128)S(1)}, u32[]{:S(2)}) copy-start(f32[320,640]{1,0:T(8,128)S(1)} %get-tuple-element.212) | copy-start | bytes 2457604
  (77 other events, 170.4 us)
Sparse Core Ops, SparseCore 0:
  45.7 68.6 all-gather.4
  115.9 124.6 all-gather.2
  274.5 65.7 reduce-scatter.8
  342.4 65.6 reduce-scatter.6
  440.4 65.4 reduce-scatter.10
  508.1 182.1 reduce-scatter.4
